TPU v7x, 32 devices: a whole 2x2x4 slice. The times are simulated.
32 devices in a mesh: dp: 2 (over x), y: 4 (over z), x: 4 (over y, core).
Axes of the slice: x: 2, y: 2, z: 4, core: 2. Of those that a mesh axis runs over, the one named last changes fastest.
Arguments:
- hidden: bfloat16 [128, 5120], P('dp', 'x'), parts along dimension 0
- positions: int32 [128], P('dp'), parts along dimension 0
- k_cache: bfloat16 [2, 128, 128, 8, 128], P(None, ('dp', 'x'), None, 'y'), parts along dimension 1
- v_cache: bfloat16 [2, 128, 128, 8, 128], P(None, ('dp', 'x'), None, 'y'), parts along dimension 1
- g_attn: bfloat16 [2, 5120], P(None, 'x')
- g_mlp: bfloat16 [2, 5120], P(None, 'x')
- q_gain: bfloat16 [2, 128], replicated
- k_gain: bfloat16 [2, 128], replicated
- w_q: bfloat16 [2, 5120, 5120], P(None, 'x', 'y')
- w_k: bfloat16 [2, 5120, 1024], P(None, 'x', 'y')
- w_v: bfloat16 [2, 5120, 1024], P(None, 'x', 'y')
- w_o: bfloat16 [2, 5120, 5120], P(None, 'y', 'x')
- w_gate: bfloat16 [2, 5120, 17408], P(None, 'x', 'y')
- w_up: bfloat16 [2, 5120, 17408], P(None, 'x', 'y')
- w_down: bfloat16 [2, 17408, 5120], P(None, 'y', 'x')
Outputs:
- output 1: bfloat16 [128, 5120], P('dp', 'x'), parts along dimension 0
- output 2: bfloat16 [2, 128, 128, 8, 128], P(None, ('dp', 'x'), None, 'y'), parts along dimension 1
- output 3: bfloat16 [2, 128, 128, 8, 128], P(None, ('dp', 'x'), None, 'y'), parts along dimension 1
There are 2 independent parts. A program takes and returns all parts, laid end to end along the dimension named above; an argument that names none is the same for every part.
All inputs are finite; a program needn't handle non-finite values.
Results may differ from a plain program's by a relative error of at most 0.02.
Values are sent between devices in bfloat16 or wider.
A program may use at most 1 GiB of HBM per device.

v0:
```python
import jax
import jax.numpy as jnp
from jax import lax
from jax.sharding import PartitionSpec as P

HEAD_DIM = 128
NORM_EPS = 1e-6
ROPE_BASE = 1000000.0


def rope_tables(positions):
    half_dim = HEAD_DIM // 2
    inv_freq = jnp.power(ROPE_BASE, -2.0 * jnp.arange(half_dim, dtype=jnp.float32) / HEAD_DIM)
    angles = positions.astype(jnp.float32)[:, None] * inv_freq[None, :]
    return jnp.cos(angles), jnp.sin(angles)


def head_norm_rope(head_vals, norm_gain, cos_tab, sin_tab):
    heads_f32 = head_vals.astype(jnp.float32)
    mean_sq = jnp.mean(heads_f32 * heads_f32, axis=-1, keepdims=True)
    normed = heads_f32 * lax.rsqrt(mean_sq + NORM_EPS) * norm_gain.astype(jnp.float32)
    half_dim = HEAD_DIM // 2
    first_half = normed[..., :half_dim]
    second_half = normed[..., half_dim:]
    cos_b = cos_tab[:, None, :]
    sin_b = sin_tab[:, None, :]
    return jnp.concatenate([first_half * cos_b - second_half * sin_b, second_half * cos_b + first_half * sin_b], axis=-1).astype(jnp.bfloat16)


def sharded_rms(hidden, norm_gain, model_dim):
    hidden_f32 = hidden.astype(jnp.float32)
    sum_sq = lax.psum(jnp.sum(hidden_f32 * hidden_f32, axis=1, keepdims=True), 'x')
    return (hidden_f32 * lax.rsqrt(sum_sq / model_dim + NORM_EPS) * norm_gain.astype(jnp.float32)).astype(jnp.bfloat16)


def cache_attention(q_rot, k_cache, v_cache, k_rot, v_proj, my_pos):
    batch_rows, q_local, head_dim = q_rot.shape
    cache_len = k_cache.shape[1]
    kv_local = k_cache.shape[2]
    slot_ids = lax.broadcasted_iota(jnp.int32, (1, cache_len), 1)
    slot_hit = (slot_ids == my_pos[:, None])[:, :, None, None]
    k_new = jnp.where(slot_hit, k_rot[:, None], k_cache)
    v_new = jnp.where(slot_hit, v_proj[:, None], v_cache)
    q_grouped = q_rot.reshape(batch_rows, kv_local, q_local // kv_local, head_dim)
    scores = jnp.einsum('bkge,blke->bkgl', q_grouped, k_new, preferred_element_type=jnp.float32) * (HEAD_DIM ** -0.5)
    valid_slot = (slot_ids <= my_pos[:, None])[:, None, None, :]
    scores = jnp.where(valid_slot, scores, -1e30)
    att_probs = jax.nn.softmax(scores, axis=-1).astype(jnp.bfloat16)
    attn_heads = jnp.einsum('bkgl,blke->bkge', att_probs, v_new, preferred_element_type=jnp.float32).astype(jnp.bfloat16)
    return attn_heads.reshape(batch_rows, q_local * head_dim), k_new, v_new


def solution(mesh):
    group_size = mesh.shape['x']
    cache_spec = P(None, ('dp', 'x'), None, 'y', None)
    col_spec = P(None, 'x', 'y')
    row_spec = P(None, 'y', 'x')
    in_specs = (P('dp', 'x'), P('dp'), cache_spec, cache_spec, P(None, 'x'), P(None, 'x'), P(), P(), col_spec, col_spec, col_spec, row_spec, col_spec, col_spec, row_spec)
    out_specs = (P('dp', 'x'), cache_spec, cache_spec)

    def device_step(hidden, positions, k_cache, v_cache, g_attn, g_mlp, q_gain, k_gain, w_q, w_k, w_v, w_o, w_gate, w_up, w_down):
        model_dim = hidden.shape[1] * group_size
        local_batch = k_cache.shape[1]
        kv_local = k_cache.shape[3]
        q_cols = w_q.shape[2]
        kv_cols = w_k.shape[2]
        ffn_local = w_gate.shape[2]
        my_pos = lax.dynamic_slice_in_dim(positions, lax.axis_index('x') * local_batch, local_batch)
        cos_tab, sin_tab = rope_tables(my_pos)
        k_list = []
        v_list = []
        for layer_idx in range(k_cache.shape[0]):
            normed = sharded_rms(hidden, g_attn[layer_idx], model_dim)
            proj_parts = jnp.concatenate([
                jnp.dot(normed, w_q[layer_idx], preferred_element_type=jnp.float32).astype(jnp.bfloat16),
                jnp.dot(normed, w_k[layer_idx], preferred_element_type=jnp.float32).astype(jnp.bfloat16),
                jnp.dot(normed, w_v[layer_idx], preferred_element_type=jnp.float32).astype(jnp.bfloat16)], axis=1)
            proj_sum = lax.psum_scatter(proj_parts, 'x', scatter_dimension=0, tiled=True)
            q_proj = proj_sum[:, :q_cols].reshape(local_batch, q_cols // HEAD_DIM, HEAD_DIM)
            k_proj = proj_sum[:, q_cols:q_cols + kv_cols].reshape(local_batch, kv_local, HEAD_DIM)
            v_proj = proj_sum[:, q_cols + kv_cols:].reshape(local_batch, kv_local, HEAD_DIM)
            q_rot = head_norm_rope(q_proj, q_gain[layer_idx], cos_tab, sin_tab)
            k_rot = head_norm_rope(k_proj, k_gain[layer_idx], cos_tab, sin_tab)
            attn_local, k_new, v_new = cache_attention(q_rot, k_cache[layer_idx], v_cache[layer_idx], k_rot, v_proj, my_pos)
            attn_all = lax.all_gather(attn_local, 'x', axis=0, tiled=True)
            attn_out = lax.psum(jnp.dot(attn_all, w_o[layer_idx], preferred_element_type=jnp.float32).astype(jnp.bfloat16), 'y')
            mid_hidden = (hidden.astype(jnp.float32) + attn_out.astype(jnp.float32)).astype(jnp.bfloat16)
            normed_mlp = sharded_rms(mid_hidden, g_mlp[layer_idx], model_dim)
            gate_up = lax.psum(jnp.concatenate([
                jnp.dot(normed_mlp, w_gate[layer_idx], preferred_element_type=jnp.float32).astype(jnp.bfloat16),
                jnp.dot(normed_mlp, w_up[layer_idx], preferred_element_type=jnp.float32).astype(jnp.bfloat16)], axis=1), 'x')
            act_val = (jax.nn.silu(gate_up[:, :ffn_local].astype(jnp.float32)) * gate_up[:, ffn_local:].astype(jnp.float32)).astype(jnp.bfloat16)
            mlp_out = lax.psum(jnp.dot(act_val, w_down[layer_idx], preferred_element_type=jnp.float32).astype(jnp.bfloat16), 'y')
            hidden = (mid_hidden.astype(jnp.float32) + mlp_out.astype(jnp.float32)).astype(jnp.bfloat16)
            k_list.append(k_new)
            v_list.append(v_new)
        return hidden, jnp.stack(k_list), jnp.stack(v_list)

    return jax.shard_map(device_step, mesh=mesh, in_specs=in_specs, out_specs=out_specs, check_vma=False)
```

profile of v0, /device:TPU:0, one launch (start us, length us, event | category | flops | bytes accessed | tf_op | source)
XLA Modules:
  0.0 395.4 jit_solution(6167517950895341909)
XLA Ops:
  7.2 1.1 fusion.98
  8.3 8.4 %psum.70 = f32[64,1]{0,1:T(1,128)S(1)} all-reduce(f32[64,1]{0,1:T(1,128)S(1)} %bitcast.112), channel_id=1, replica_groups=mesh['dp'=2,'y'=4,'x'=4] {'x'}, use_global_device_ids=true, to_apply=%region_1.0 | all-reduce | flops 64 | bytes 512 | tf_op jit(solution)/shard_map/psum | solution.py:32
  16.8 0.8 convert_reduce_fusion.3
  17.6 1.4 convolution_convert_fusion.5
  19.0 1.5 convolution_convert_fusion.4
  20.5 2.7 fusion.44
  23.2 0.7 pad_maximum_fusion.4
  24.2 0.1 multiply_cosine_fusion
  24.4 19.9 %reduce-scatter.3.cloned.1.call-done = bf16[16,1792]{1,0:T(8,128)(2,1)} async-done(((bf16[64,1792]{1,0:T(8,128)(2,1)}), bf16[16,1792]{1,0:T(8,128)(2,1)}) %reduce-scatter.3.cloned.1.call-update) | async-done | bytes 57360 | tf_op jit(solution)/shard_map/reduce_scatter | solution.py:78
  44.3 0.7 slice_convert_fusion.3
  45.1 0.8 slice_convert_fusion.1
  45.9 0.1 multiply_reduce_fusion.1
  46.1 0.1 multiply_multiply_fusion.1
  46.3 0.1 subtract_convert_fusion.1
  46.6 5.5 %broadcast_select_fusion.7 = (bf16[16,128,2,128]{3,2,1,0:T(2,128)(2,1)S(1)}, bf16[16,128,2,128]{3,2,1,0:T(2,128)(2,1)S(1)}) fusion(pred[16,128]{1,0:T(8,128)(4,1)S(1)} %get-tuple-element.42, bf16[2,16,128,2,128]{4,3,2,1,0:T(2,128)(2,1)S(1)} %copy-done, bf16[16,2,128]{2,1,0:T(2,128)(2,1)S(1)} %pad_maximum_fusion.6, bf16[2,16,128,2,128]{4,3,2,1,0:T(2,128)(2,1)} %param.18, ...), kind=kLoop, calls=%fused_computation.51 | loop fusion | flops 1048576 | bytes 4212736 | tf_op jit(solution)/shard_map/jit(_where)/select_n | solution.py:42
  52.1 0.7 fusion.66
  52.8 0.2 fusion.136
  53.0 1.2 convolution_convert_fusion.1
  54.3 0.9 reshape.216
  55.2 5.5 %all_gather.6 = bf16[64,1280]{1,0:T(8,128)(2,1)S(1)} all-gather(bf16[16,1280]{1,0:T(8,128)(2,1)S(1)} %reshape.216), channel_id=1, replica_groups=mesh['dp'=2,'y'=4,'x'=4] {'x'}, dimensions={0}, use_global_device_ids=true | all-gather | bytes 204800 | tf_op jit(solution)/shard_map/all_gather | solution.py:85
  60.7 3.3 fusion.47
  64.1 34.7 %all-reduce.7.cloned.1.call-done = bf16[64,1280]{1,0:T(8,128)(2,1)} async-done(((bf16[64,1280]{1,0:T(8,128)(2,1)}), bf16[64,1280]{1,0:T(8,128)(2,1)}) %all-reduce.7.cloned.1.call-update) | async-done | bytes 163856 | tf_op jit(solution)/shard_map/psum | solution.py:86
  98.8 1.1 fusion.102
  99.9 5.7 %psum.72 = f32[64,1]{0,1:T(1,128)S(1)} all-reduce(f32[64,1]{0,1:T(1,128)S(1)} %bitcast.111), channel_id=1, replica_groups=mesh['dp'=2,'y'=4,'x'=4] {'x'}, use_global_device_ids=true, to_apply=%region_9.10 | all-reduce | flops 64 | bytes 512 | tf_op jit(solution)/shard_map/psum | solution.py:32
  105.6 6.3 %fusion.23 = bf16[64,4352]{1,0:T(8,128)(2,1)S(1)} fusion(bf16[2,1280,4352]{2,1,0:T(8,128)(2,1)} %param.28, bf16[64,1280]{1,0:T(8,128)(2,1)S(1)} %get-tuple-element.10, f32[1280]{0:T(1024)S(1)} %get-tuple-element.4, f32[64]{0:T(128)S(1)} %rsqrt_bitcast_fusion.2), kind=kOutput, calls=%fused_computation.21 | convolution fusion | flops 713637888 | bytes 11867392 | tf_op jit(solution)/shard_map/dot_general | solution.py:91
  111.9 6.3 %fusion.20 = bf16[64,4352]{1,0:T(8,128)(2,1)S(1)} fusion(bf16[2,1280,4352]{2,1,0:T(8,128)(2,1)} %param.27, bf16[64,1280]{1,0:T(8,128)(2,1)S(1)} %get-tuple-element.10, f32[1280]{0:T(1024)S(1)} %get-tuple-element.4, f32[64]{0:T(128)S(1)} %rsqrt_bitcast_fusion.2), kind=kOutput, calls=%fused_computation.20 | convolution fusion | flops 713637888 | bytes 11867392 | tf_op jit(solution)/shard_map/dot_general | solution.py:90
  118.2 1.1 pad_maximum_fusion.2
  119.3 36.8 %all-reduce.9.cloned.1.call-done = bf16[64,8704]{1,0:T(8,128)(2,1)} async-done(((bf16[64,8704]{1,0:T(8,128)(2,1)}), bf16[64,8704]{1,0:T(8,128)(2,1)}) %all-reduce.9.cloned.1.call-update) | async-done | bytes 1114128 | tf_op jit(solution)/shard_map/psum | solution.py:89
  156.1 7.2 %fusion.56 = bf16[64,1280]{1,0:T(8,128)(2,1)} fusion(bf16[2,4352,1280]{2,1,0:T(8,128)(2,1)} %param.29, bf16[64,8704]{1,0:T(8,128)(2,1)} %all-reduce.9.cloned.1.call-done), kind=kOutput, calls=%fused_computation.40 | convolution fusion | flops 715341824 | bytes 12419072 | tf_op jit(solution)/shard_map/dot_general | solution.py:93
  163.5 35.1 %all-reduce.11.cloned.1.call-done = bf16[64,1280]{1,0:T(8,128)(2,1)} async-done(((bf16[64,1280]{1,0:T(8,128)(2,1)}), bf16[64,1280]{1,0:T(8,128)(2,1)}) %all-reduce.11.cloned.1.call-update) | async-done | bytes 163856 | tf_op jit(solution)/shard_map/psum | solution.py:93
  198.6 1.1 fusion.106
  199.7 5.7 %psum.75 = f32[64,1]{0,1:T(1,128)S(1)} all-reduce(f32[64,1]{0,1:T(1,128)S(1)} %bitcast.113), channel_id=1, replica_groups=mesh['dp'=2,'y'=4,'x'=4] {'x'}, use_global_device_ids=true, to_apply=%region_13.14 | all-reduce | flops 64 | bytes 512 | tf_op jit(solution)/shard_map/psum | solution.py:32
  205.4 1.0 fusion.108
  206.4 1.3 convolution_convert_fusion.2
  207.7 1.3 convolution_convert_fusion.3
  209.1 2.6 fusion.50
  211.7 0.7 pad_maximum_fusion.5
  212.5 20.0 %reduce-scatter.5.cloned.1.call-done = bf16[16,1792]{1,0:T(8,128)(2,1)} async-done(((bf16[64,1792]{1,0:T(8,128)(2,1)}), bf16[16,1792]{1,0:T(8,128)(2,1)}) %reduce-scatter.5.cloned.1.call-update) | async-done | bytes 57360 | tf_op jit(solution)/shard_map/reduce_scatter | solution.py:78
  232.5 0.7 slice_convert_fusion.2
  233.2 0.1 multiply_reduce_fusion.2
  233.4 0.1 subtract_convert_fusion.2
  233.5 0.8 slice_convert_fusion
  234.3 0.1 multiply_reduce_fusion
  234.4 0.1 multiply_multiply_fusion
  234.6 0.1 subtract_convert_fusion
  234.9 5.5 %broadcast_select_fusion.5 = (bf16[16,128,2,128]{3,2,1,0:T(2,128)(2,1)S(1)}, bf16[16,128,2,128]{3,2,1,0:T(2,128)(2,1)S(1)}) fusion(pred[16,128]{1,0:T(8,128)(4,1)S(1)} %get-tuple-element.42, bf16[2,16,128,2,128]{4,3,2,1,0:T(2,128)(2,1)S(1)} %copy-done, bf16[16,2,128]{2,1,0:T(2,128)(2,1)S(1)} %pad_maximum_fusion.7, bf16[2,16,128,2,128]{4,3,2,1,0:T(2,128)(2,1)} %param.18, ...), kind=kLoop, calls=%fused_computation.49 | loop fusion | flops 1048576 | bytes 4212736 | tf_op jit(solution)/shard_map/jit(_where)/select_n | solution.py:42
  240.3 0.7 fusion.67
  241.0 0.2 fusion.137
  241.3 1.2 convolution_convert_fusion
  242.5 0.9 reshape.217
  243.4 5.7 %all_gather.7 = bf16[64,1280]{1,0:T(8,128)(2,1)S(1)} all-gather(bf16[16,1280]{1,0:T(8,128)(2,1)S(1)} %reshape.217), channel_id=1, replica_groups=mesh['dp'=2,'y'=4,'x'=4] {'x'}, dimensions={0}, use_global_device_ids=true | all-gather | bytes 204800 | tf_op jit(solution)/shard_map/all_gather | solution.py:85
  249.1 3.3 fusion.53
  252.5 34.7 %all-reduce.13.cloned.1.call-done = bf16[64,1280]{1,0:T(8,128)(2,1)} async-done(((bf16[64,1280]{1,0:T(8,128)(2,1)}), bf16[64,1280]{1,0:T(8,128)(2,1)}) %all-reduce.13.cloned.1.call-update) | async-done | bytes 163856 | tf_op jit(solution)/shard_map/psum | solution.py:86
  287.2 1.1 fusion.110
  288.3 5.7 %psum.77 = f32[64,1]{0,1:T(1,128)S(1)} all-reduce(f32[64,1]{0,1:T(1,128)S(1)} %bitcast.114), channel_id=1, replica_groups=mesh['dp'=2,'y'=4,'x'=4] {'x'}, use_global_device_ids=true, to_apply=%region_21.22 | all-reduce | flops 64 | bytes 512 | tf_op jit(solution)/shard_map/psum | solution.py:32
  294.0 6.3 %fusion.29 = bf16[64,4352]{1,0:T(8,128)(2,1)S(1)} fusion(bf16[2,1280,4352]{2,1,0:T(8,128)(2,1)} %param.28, bf16[64,1280]{1,0:T(8,128)(2,1)S(1)} %get-tuple-element.8, f32[1280]{0:T(1024)S(1)} %get-tuple-element.3, f32[64]{0:T(128)S(1)} %rsqrt_bitcast_fusion), kind=kOutput, calls=%fused_computation.23 | convolution fusion | flops 713637888 | bytes 11867392 | tf_op jit(solution)/shard_map/dot_general | solution.py:91
  300.2 6.3 %fusion.26 = bf16[64,4352]{1,0:T(8,128)(2,1)S(1)} fusion(bf16[2,1280,4352]{2,1,0:T(8,128)(2,1)} %param.27, bf16[64,1280]{1,0:T(8,128)(2,1)S(1)} %get-tuple-element.8, f32[1280]{0:T(1024)S(1)} %get-tuple-element.3, f32[64]{0:T(128)S(1)} %rsqrt_bitcast_fusion), kind=kOutput, calls=%fused_computation.22 | convolution fusion | flops 713637888 | bytes 11867392 | tf_op jit(solution)/shard_map/dot_general | solution.py:90
  306.5 1.1 pad_maximum_fusion.3
  307.7 7.8 %broadcast_select_fusion.1 = (bf16[1,16,128,2,128]{4,3,2,1,0:T(2,128)(2,1)S(1)}, bf16[1,16,128,2,128]{4,3,2,1,0:T(2,128)(2,1)}, bf16[1,16,128,2,128]{4,3,2,1,0:T(2,128)(2,1)}, bf16[1,16,128,2,128]{4,3,2,1,0:T(2,128)(2,1)}) fusion(pred[16,128]{1,0:T(8,128)(4,1)S(1)} %get-tuple-element.42, bf16[2,16,128,2,128]{4,3,2,1,0:T(2,128)(2,1)} %param.18, ...), kind=kLoop, calls=%fused_computation.45 | loop fusion | flops 2097152 | bytes 8423424 | tf_op jit(solution)/shard_map/jit(_where)/select_n | solution.py:43
  315.6 29.0 %all-reduce.15.cloned.1.call-done = bf16[64,8704]{1,0:T(8,128)(2,1)} async-done(((bf16[64,8704]{1,0:T(8,128)(2,1)}), bf16[64,8704]{1,0:T(8,128)(2,1)}) %all-reduce.15.cloned.1.call-update) | async-done | bytes 1114128 | tf_op jit(solution)/shard_map/psum | solution.py:89
  344.5 7.2 %fusion.59 = bf16[64,1280]{1,0:T(8,128)(2,1)} fusion(bf16[2,4352,1280]{2,1,0:T(8,128)(2,1)} %param.29, bf16[64,8704]{1,0:T(8,128)(2,1)} %all-reduce.15.cloned.1.call-done), kind=kOutput, calls=%fused_computation.41 | convolution fusion | flops 715341824 | bytes 12419072 | tf_op jit(solution)/shard_map/dot_general | solution.py:93
  351.8 8.2 %pad_maximum_fusion = (bf16[2,16,128,2,128]{4,3,2,1,0:T(2,128)(2,1)}, bf16[2,16,128,2,128]{4,3,2,1,0:T(2,128)(2,1)}) fusion(bf16[1,16,128,2,128]{4,3,2,1,0:T(2,128)(2,1)S(1)} %copy-done.2, bf16[1,16,128,2,128]{4,3,2,1,0:T(2,128)(2,1)} %get-tuple-element.30, bf16[1,16,128,2,128]{4,3,2,1,0:T(2,128)(2,1)S(1)} %copy-done.1, ...), kind=kLoop, calls=%fused_computation.42 | loop fusion | flops 2097152 | bytes 8388608 | tf_op jit(solution)/shard_map/stack | solution.py:97
  360.0 26.9 %all-reduce.17.cloned.1.call-done = bf16[64,1280]{1,0:T(8,128)(2,1)} async-done(((bf16[64,1280]{1,0:T(8,128)(2,1)}), bf16[64,1280]{1,0:T(8,128)(2,1)}) %all-reduce.17.cloned.1.call-update) | async-done | bytes 163856 | tf_op jit(solution)/shard_map/psum | solution.py:93
  387.0 1.6 fusion.113
  (68 shorter events, 1.5 us)
Async XLA Ops:
  7.2 13.3 %copy-start.4 = (bf16[64,1280]{1,0:T(8,128)(2,1)S(1)}, bf16[64,1280]{1,0:T(8,128)(2,1)}, u32[]{:S(2)}) copy-start(bf16[64,1280]{1,0:T(8,128)(2,1)} %param.15) | copy-start | bytes 491524
  7.2 37.1 %reduce-scatter.3.cloned.1.call-start = ((), (), s32[]{:S(2)}) async-start(), calls=%async_computation.2 | async-start | bytes 286720 | tf_op jit(solution)/shard_map/reduce_scatter | solution.py:78
  20.5 3.5 copy-start.6
  20.5 3.5 copy-start.7
  20.5 3.5 copy-start.8
  23.2 23.4 %copy-start = (bf16[2,16,128,2,128]{4,3,2,1,0:T(2,128)(2,1)S(1)}, bf16[2,16,128,2,128]{4,3,2,1,0:T(2,128)(2,1)}, u32[]{:S(2)}) copy-start(bf16[2,16,128,2,128]{4,3,2,1,0:T(2,128)(2,1)} %param.17) | copy-start | bytes 6291460
  23.9 74.9 %all-reduce.7.cloned.1.call-start = ((), (), s32[]{:S(2)}) async-start(), calls=%async_computation.3 | async-start | bytes 327680 | tf_op jit(solution)/shard_map/psum | solution.py:86
  60.7 3.4 copy-start.5
  64.0 92.1 %all-reduce.9.cloned.1.call-start = ((), (), s32[]{:S(2)}) async-start(), calls=%async_computation.4 | async-start | bytes 2228224 | tf_op jit(solution)/shard_map/psum | solution.py:89
  119.2 79.4 %all-reduce.11.cloned.1.call-start = ((), (), s32[]{:S(2)}) async-start(), calls=%async_computation.5 | async-start | bytes 327680 | tf_op jit(solution)/shard_map/psum | solution.py:93
  163.4 69.1 %reduce-scatter.5.cloned.1.call-start = ((), (), s32[]{:S(2)}) async-start(), calls=%async_computation.6 | async-start | bytes 286720 | tf_op jit(solution)/shard_map/reduce_scatter | solution.py:78
  212.4 74.8 %all-reduce.13.cloned.1.call-start = ((), (), s32[]{:S(2)}) async-start(), calls=%async_computation.7 | async-start | bytes 327680 | tf_op jit(solution)/shard_map/psum | solution.py:86
  249.1 38.1 %copy-start.3 = (bf16[64,1280]{1,0:T(8,128)(2,1)S(1)}, bf16[64,1280]{1,0:T(8,128)(2,1)}, u32[]{:S(2)}) copy-start(bf16[64,1280]{1,0:T(8,128)(2,1)} %all-reduce.11.cloned.1.call-done) | copy-start | bytes 491524
  252.4 92.1 %all-reduce.15.cloned.1.call-start = ((), (), s32[]{:S(2)}) async-start(), calls=%async_computation.8 | async-start | bytes 2228224 | tf_op jit(solution)/shard_map/psum | solution.py:89
  307.6 79.3 %all-reduce.17.cloned.1.call-start = ((), (), s32[]{:S(2)}) async-start(), calls=%async_computation.9 | async-start | bytes 327680 | tf_op jit(solution)/shard_map/psum | solution.py:93
  315.5 36.3 %copy-start.1 = (bf16[1,16,128,2,128]{4,3,2,1,0:T(2,128)(2,1)S(1)}, bf16[1,16,128,2,128]{4,3,2,1,0:T(2,128)(2,1)}, u32[]{:S(2)}) copy-start(bf16[1,16,128,2,128]{4,3,2,1,0:T(2,128)(2,1)} %get-tuple-element.14) | copy-start | bytes 3145732
  315.5 36.3 %copy-start.2 = (bf16[1,16,128,2,128]{4,3,2,1,0:T(2,128)(2,1)S(1)}, bf16[1,16,128,2,128]{4,3,2,1,0:T(2,128)(2,1)}, u32[]{:S(2)}) copy-start(bf16[1,16,128,2,128]{4,3,2,1,0:T(2,128)(2,1)} %get-tuple-element.29) | copy-start | bytes 3145732
Sparse Core Ops, SparseCore 0:
  24.1 20.1 reduce-scatter.2
  64.1 34.6 all-reduce.6
  119.4 36.7 all-reduce.8
  163.5 35.0 all-reduce.10
  212.5 19.8 reduce-scatter.4
  252.5 34.5 all-reduce.12
  307.8 36.7 all-reduce.14
  351.9 34.9 all-reduce.16
where the time goes:
time: 397 us; the launch traced here: 395 us
  waiting for transfers between devices  237 us (60%)
  matrix products  60.9 us (15%)
  other arithmetic  43.5 us (11%)
  blocking collectives  36.6 us (9%)
  between operations  14.6 us (4%)
    psum x2, waiting for transfers between devices, device_step(): lax.psum(jnp.dot(attn_all, w_o[layer_idx], preferred_element_type=jnp.flo...  69.4 us
    psum x2, waiting for transfers between devices, device_step(): lax.psum(jnp.concatenate([jnp.dot(normed_mlp, w_gate[layer_idx], preferre...  65.8 us
    psum x2, waiting for transfers between devices, device_step(): lax.psum(jnp.dot(act_val, w_down[layer_idx], preferred_element_type=jnp.f...  62.1 us
    reduce_scatter x2, waiting for transfers between devices, device_step(): lax.psum_scatter(proj_parts, 'x', scatter_dimension=0, tiled=True)  39.9 us
    psum x4, blocking collectives, sharded_rms(): lax.psum(jnp.sum(hidden_f32 * hidden_f32, axis=1, keepdims=True), 'x')  25.4 us
    dot_general x2, matrix products, device_step(): jnp.dot(act_val, w_down[layer_idx], preferred_element_type=jnp.float32)  14.5 us
    dot_general x2, matrix products, device_step(): jnp.dot(normed_mlp, w_gate[layer_idx], preferred_element_type=jnp.float32)  12.6 us
    dot_general x2, matrix products, device_step(): jnp.dot(normed_mlp, w_up[layer_idx], preferred_element_type=jnp.float32)  12.6 us
  transfers between devices with their start and end apart: 8, of which 8 were waited for; matrix products, arithmetic and copies ran while one was open for 4% of the time, Pallas kernels for 0%

commit v1 on v0

v1 whole, which is shorter than its diff:
```python
import functools

import jax
import jax.numpy as jnp
from jax import lax
from jax.experimental import pallas as pl
from jax.experimental.pallas import tpu as pltpu
from jax.sharding import PartitionSpec as P

HEAD_DIM = 128
NORM_EPS = 1e-6
ROPE_BASE = 1000000.0
TILE = 256
CHUNKS = 4
MESH = pl.DeviceIdType.MESH
F32 = jnp.float32
BF16 = jnp.bfloat16
N_REMOTE = 160
N_LOCAL = 48


def rope_tables(positions):
    half_dim = HEAD_DIM // 2
    inv_freq = jnp.power(ROPE_BASE, -2.0 * jnp.arange(half_dim, dtype=F32) / HEAD_DIM)
    angles = positions.astype(F32)[:, None] * inv_freq[None, :]
    return jnp.cos(angles), jnp.sin(angles)


def split_tiles(n_tiles, n_chunks):
    sizes = [n_tiles // n_chunks + (1 if i < n_tiles % n_chunks else 0) for i in range(n_chunks)]
    starts = [sum(sizes[:i]) for i in range(n_chunks)]
    return [(s * TILE, z * TILE) for s, z in zip(starts, sizes) if z]


def step_kernel(dims, *refs):
    (layers, n_y, n_x, rows, depth, q_cols, kv_cols, ffn) = dims
    (hid_ref, pos_ref, cos_ref, sin_ref, ga_ref, gm_ref, qg_ref, kg_ref, kc_ref, vc_ref,
     wq_ref, wk_ref, wv_ref, wo_ref, wg_ref, wu_ref, wd_ref,
     hid_out, kc_out, vc_out,
     wqkv, wo, wg, wu, wd, kbuf, vbuf, n_buf, stat, qkv_part, qkv_recv, q_rows, o_rows, attn_all,
     ar_part, ar_recv, h_all, gu_part, gu_pair, gu_send, gu_recv, act_all, acc,
     send_sem, recv_sem, local_sem) = refs
    batch = n_y * rows
    cols_qkv = q_cols + 2 * kv_cols
    q_heads = q_cols // HEAD_DIM
    kv_heads = kv_cols // HEAD_DIM
    group = q_heads // kv_heads
    chunks = split_tiles(ffn // TILE, CHUNKS)
    model_dim = depth * n_x
    slots2 = kbuf.shape[2]

    y = lax.axis_index("y")
    x = lax.axis_index("x")
    chip = x // 2
    core = x % 2
    partner = 2 * chip + (1 - core)
    across = 2 * (1 - chip) + core

    counter = {"remote": 0, "local": 0}
    sent = []
    stored = []

    def remote(src, dst, to_y, to_x):
        i = counter["remote"]
        counter["remote"] += 1
        copy = pltpu.make_async_remote_copy(
            src_ref=src, dst_ref=dst, send_sem=send_sem.at[i], recv_sem=recv_sem.at[i],
            device_id={"y": to_y, "x": to_x}, device_id_type=MESH)
        copy.start()
        sent.append(copy)
        return copy

    def local(src, dst):
        i = counter["local"]
        counter["local"] += 1
        copy = pltpu.make_async_copy(src, dst, local_sem.at[i])
        copy.start()
        return copy

    def load_qkv(layer):
        return [local(wq_ref.at[layer], wqkv.at[:, 0:q_cols]),
                local(wk_ref.at[layer], wqkv.at[:, q_cols:q_cols + kv_cols]),
                local(wv_ref.at[layer], wqkv.at[:, q_cols + kv_cols:cols_qkv])]

    def load_o(layer):
        return [local(wo_ref.at[layer], wo)]

    def load_gate_up(layer, j):
        cols = pl.ds(chunks[j][0], chunks[j][1])
        return [local(wg_ref.at[layer, :, cols], wg.at[:, cols]),
                local(wu_ref.at[layer, :, cols], wu.at[:, cols])]

    def load_down(layer, j):
        cols = pl.ds(chunks[j][0], chunks[j][1])
        return [local(wd_ref.at[layer, cols, :], wd.at[cols, :])]

    def load_cache(layer):
        return [local(kc_ref.at[layer], kbuf.at[layer]), local(vc_ref.at[layer], vbuf.at[layer])]

    def wait_all(copies):
        for copy in copies:
            copy.wait()

    row_i = lax.broadcasted_iota(jnp.int32, (rows, HEAD_DIM), 0)
    lane_i = lax.broadcasted_iota(jnp.int32, (rows, HEAD_DIM), 1)

    def pack_rows(vals_f32, first_row):
        sums = jnp.sum(vals_f32 * vals_f32, axis=1, keepdims=True)
        return jnp.sum(jnp.where(lane_i == row_i + first_row, sums, 0.0), axis=0, keepdims=True)

    all_row = lax.broadcasted_iota(jnp.int32, (batch, HEAD_DIM), 0)
    all_lane = lax.broadcasted_iota(jnp.int32, (batch, HEAD_DIM), 1)

    def row_scales(i, count):
        total = stat[i, 0]
        for s in range(1, count):
            total = total + stat[i, s]
        scale = lax.rsqrt(total / model_dim + NORM_EPS)
        return jnp.sum(jnp.where(all_lane == all_row, scale, 0.0), axis=1, keepdims=True)

    def normalise(hidden_ref, i, count, gain_ref, layer):
        scales = row_scales(i, count)
        gain = gain_ref[...].astype(F32)[layer:layer + 1]
        vals = hidden_ref[...].reshape(batch, depth).astype(F32)
        n_buf[...] = (vals * scales * gain).astype(BF16)

    def all_reduce(i, residual_ref, with_stats):
        copies = [remote(ar_part.at[i, (y + d) % n_y], ar_recv.at[i, d], (y + d) % n_y, x) for d in (3, 2, 1)]
        total = ar_part[i, y].astype(F32)
        for copy in copies:
            copy.wait_recv()
        for d in range(1, n_y):
            total = total + ar_recv[i, d].astype(F32)
        new = (residual_ref[y].astype(F32) + total.astype(BF16).astype(F32)).astype(BF16)
        h_all[i, y] = new
        gathers = [remote(h_all.at[i, y], h_all.at[i, y], (y + d) % n_y, x) for d in (3, 2, 1)]
        stats = []
        if with_stats:
            stat[i + 1, 0] = pack_rows(new.astype(F32), y * rows)
            stats = [remote(stat.at[i + 1, 0], stat.at[i + 1, dy * n_x + dx], (y + dy) % n_y, (x + dx) % n_x)
                     for dy in (3, 2, 1, 0) for dx in range(n_x) if dy or dx]
        for copy in gathers + stats:
            copy.wait_recv()

    pending_qkv = load_qkv(0)
    barrier = pltpu.get_barrier_semaphore()
    for dy in range(n_y):
        for dx in range(n_x):
            if dy or dx:
                pl.semaphore_signal(barrier, inc=1, device_id={"y": (y + dy) % n_y, "x": (x + dx) % n_x}, device_id_type=MESH)
    own = jnp.zeros((1, HEAD_DIM), F32)
    for b in range(n_y):
        own = own + pack_rows(hid_ref[b].astype(F32), b * rows)
    stat[0, 0] = own
    pl.semaphore_wait(barrier, n_y * n_x - 1)
    first_stats = [remote(stat.at[0, 0], stat.at[0, d], y, (x + d) % n_x) for d in range(1, n_x)]
    pending_o = load_o(0)
    pending_cache = [load_cache(0)]
    pending_gu = [load_gate_up(0, j) for j in range(len(chunks))]
    pending_down = [load_down(0, j) for j in range(len(chunks))]
    pending_cache += [load_cache(layer) for layer in range(1, layers)]
    q_rows[...] = jnp.zeros_like(q_rows)
    for copy in first_stats:
        copy.wait_recv()

    cos_tab = cos_ref[...]
    sin_tab = sin_ref[...]
    slot_row = lax.broadcasted_iota(jnp.int32, (slots2, HEAD_DIM), 0)
    slot_id = slot_row // kv_heads
    head_id = slot_row % kv_heads
    score_col = lax.broadcasted_iota(jnp.int32, (16, slots2), 1)
    score_head = lax.broadcasted_iota(jnp.int32, (16, slots2), 0) // group

    residual = hid_ref
    for layer in range(layers):
        more = layer + 1 < layers
        a, m = 2 * layer, 2 * layer + 1
        normalise(residual, a, n_x if layer == 0 else n_y * n_x, ga_ref, layer)
        wait_all(pending_qkv)

        def qkv_tile(t, carry):
            cols = pl.ds(pl.multiple_of(t * TILE, TILE), TILE)
            part = jnp.dot(n_buf[...], wqkv[:, cols], preferred_element_type=F32).astype(BF16)
            qkv_part[layer, :, :, cols] = part.reshape(n_x, batch // n_x, TILE)
            return carry

        lax.fori_loop(0, cols_qkv // TILE, qkv_tile, 0)
        copies = [remote(qkv_part.at[layer, (x + d) % n_x], qkv_recv.at[layer, d], y, (x + d) % n_x) for d in (2, 3, 1)]
        if more:
            pending_qkv = load_qkv(layer + 1)
        total = qkv_part[layer, x].astype(F32)
        for copy in copies:
            copy.wait_recv()
        for d in range(1, n_x):
            total = total + qkv_recv[layer, d].astype(F32)
        proj = total.astype(BF16).astype(F32)

        def rotate(vals, gain):
            mean_sq = jnp.mean(vals * vals, axis=-1, keepdims=True)
            normed = vals * lax.rsqrt(mean_sq + NORM_EPS) * gain
            turned = normed * cos_tab + pltpu.roll(normed, HEAD_DIM // 2, 1) * sin_tab
            return turned.astype(BF16).astype(F32)

        q_gain = qg_ref[...].astype(F32)[layer:layer + 1]
        k_gain = kg_ref[...].astype(F32)[layer:layer + 1]
        n_seq = batch // n_x
        for h in range(q_heads):
            q_rows[h * n_seq:(h + 1) * n_seq, :] = rotate(proj[:, h * HEAD_DIM:(h + 1) * HEAD_DIM], q_gain)
        k_new = [rotate(proj[:, q_cols + h * HEAD_DIM:q_cols + (h + 1) * HEAD_DIM], k_gain) for h in range(kv_heads)]
        v_new = [proj[:, q_cols + kv_cols + h * HEAD_DIM:q_cols + kv_cols + (h + 1) * HEAD_DIM] for h in range(kv_heads)]

        wait_all(pending_cache[layer])
        for b in range(n_seq):
            pos = pos_ref[b]
            hit = slot_id == pos[:, :HEAD_DIM]
            for buf, new in ((kbuf, k_new), (vbuf, v_new)):
                fresh = new[0][b:b + 1]
                for h in range(1, kv_heads):
                    fresh = jnp.where(head_id == h, new[h][b:b + 1], fresh)
                buf[layer, b] = jnp.where(hit, fresh, buf[layer, b].astype(F32)).astype(BF16)
            q_b = q_rows[pl.ds(b, 16, stride=n_seq), :].astype(BF16)
            scores = lax.dot_general(q_b, kbuf[layer, b], (((1,), (1,)), ((), ())), preferred_element_type=F32) * (HEAD_DIM ** -0.5)
            valid = (score_col // kv_heads <= pos) & (score_col % kv_heads == score_head)
            valid = valid | (score_head >= kv_heads)
            scores = jnp.where(valid, scores, -1e30)
            top = jnp.max(scores, axis=1, keepdims=True)
            e = jnp.exp(scores - top)
            probs = (e / jnp.sum(e, axis=1, keepdims=True)).astype(BF16)
            o_rows[b * 16:(b + 1) * 16, :] = jnp.dot(probs, vbuf[layer, b], preferred_element_type=F32)
        stored += [local(kbuf.at[layer], kc_out.at[layer]), local(vbuf.at[layer], vc_out.at[layer])]
        for h in range(q_heads):
            attn_all[layer, x, :, h * HEAD_DIM:(h + 1) * HEAD_DIM] = o_rows[pl.ds(h, n_seq, stride=16), :].astype(BF16)
        copies = [remote(attn_all.at[layer, x], attn_all.at[layer, x], y, (x + d) % n_x) for d in (2, 3, 1)]
        wait_all(pending_o)
        for copy in copies:
            copy.wait_recv()

        def o_tile(t, carry):
            cols = pl.ds(pl.multiple_of(t * TILE, TILE), TILE)
            part = jnp.dot(attn_all[layer].reshape(batch, q_cols), wo[:, cols], preferred_element_type=F32).astype(BF16)
            ar_part[a, :, :, cols] = part.reshape(n_y, rows, TILE)
            return carry

        lax.fori_loop(0, depth // TILE, o_tile, 0)
        if more:
            pending_o = load_o(layer + 1)
        all_reduce(a, residual, True)

        normalise(h_all.at[a], a + 1, n_y * n_x, gm_ref, layer)
        to_pair, to_across, own_gather, across_gather, forward = {}, {}, {}, {}, {}

        def project(j):
            wait_all(pending_gu[j])
            start, width = chunks[j]

            def tile(t, carry):
                cols = pl.ds(pl.multiple_of(start + t * TILE, TILE), TILE)
                gate = jnp.dot(n_buf[...], wg[:, cols], preferred_element_type=F32).astype(BF16)
                up = jnp.dot(n_buf[...], wu[:, cols], preferred_element_type=F32).astype(BF16)
                gu_part[layer, 0, :, :, :, cols] = gate.reshape(2, 2, rows, TILE)
                gu_part[layer, 1, :, :, :, cols] = up.reshape(2, 2, rows, TILE)
                return carry

            lax.fori_loop(0, width // TILE, tile, 0)
            cols = pl.ds(start, width)
            to_pair[j] = remote(gu_part.at[layer, :, :, 1 - core, :, cols], gu_pair.at[layer, :, :, :, cols], y, partner)
            if more:
                pending_gu[j] = load_gate_up(layer + 1, j)

        def cross(j):
            cols = pl.ds(*chunks[j])
            to_pair[j].wait_recv()
            pair = gu_part[layer, :, 1 - chip, core, :, cols].astype(F32) + gu_pair[layer, :, 1 - chip, :, cols].astype(F32)
            gu_send[layer, :, :, cols] = pair.astype(BF16)
            to_across[j] = remote(gu_send.at[layer, :, :, cols], gu_recv.at[layer, :, :, cols], y, across)

        def activate(j):
            cols = pl.ds(*chunks[j])
            to_across[j].wait_recv()
            gate_up = (gu_part[layer, :, chip, core, :, cols].astype(F32) + gu_pair[layer, :, chip, :, cols].astype(F32)
                       + gu_recv[layer, :, :, cols].astype(F32)).astype(BF16).astype(F32)
            act_all[layer, x, :, cols] = (jax.nn.silu(gate_up[0]) * gate_up[1]).astype(BF16)
            mine = act_all.at[layer, x, :, cols]
            across_gather[j] = remote(mine, mine, y, across)
            own_gather[j] = remote(mine, mine, y, partner)

        def pass_on(j):
            cols = pl.ds(*chunks[j])
            across_gather[j].wait_recv()
            theirs = act_all.at[layer, across, :, cols]
            forward[j] = remote(theirs, theirs, y, partner)

        def down(j):
            own_gather[j].wait_recv()
            forward[j].wait_recv()
            wait_all(pending_down[j])
            start, width = chunks[j]

            def tile(t, carry):
                cols = pl.ds(pl.multiple_of(t * TILE, TILE), TILE)
                vals = act_all[layer, :, :, pl.ds(start, width)].reshape(batch, width)
                part = jnp.dot(vals, wd[pl.ds(start, width), cols], preferred_element_type=F32)
                if j:
                    part = part + acc[:, cols]
                if j < len(chunks) - 1:
                    acc[:, cols] = part
                else:
                    ar_part[m, :, :, cols] = part.astype(BF16).reshape(n_y, rows, TILE)
                return carry

            lax.fori_loop(0, depth // TILE, tile, 0)
            if more:
                pending_down[j] = load_down(layer + 1, j)

        phases = (project, cross, activate, pass_on, down)
        for stage in range(len(chunks) + len(phases) - 1):
            for lag, phase in enumerate(phases):
                if 0 <= stage - lag < len(chunks):
                    phase(stage - lag)
        all_reduce(m, h_all.at[a], more)
        residual = h_all.at[m]

    hid_out[...] = residual[...]
    for copy in sent:
        copy.wait_send()
    wait_all(stored)


def solution(mesh):
    n_x, n_y = mesh.shape['x'], mesh.shape['y']
    cache_spec = P(None, ('dp', 'x'), None, 'y', None)
    col_spec = P(None, 'x', 'y')
    row_spec = P(None, 'y', 'x')
    in_specs = (P('dp', 'x'), P('dp'), cache_spec, cache_spec, P(None, 'x'), P(None, 'x'), P(), P(), col_spec, col_spec, col_spec, row_spec, col_spec, col_spec, row_spec)
    out_specs = (P('dp', 'x'), cache_spec, cache_spec)

    def device_step(hidden, positions, k_cache, v_cache, g_attn, g_mlp, q_gain, k_gain, w_q, w_k, w_v, w_o, w_gate, w_up, w_down):
        batch, depth = hidden.shape
        layers, n_seq, slots, kv_heads, _ = k_cache.shape
        q_cols, kv_cols, ffn = w_q.shape[2], w_k.shape[2], w_gate.shape[2]
        rows = batch // n_y
        slots2 = slots * kv_heads
        my_pos = lax.dynamic_slice_in_dim(positions, lax.axis_index('x') * n_seq, n_seq)
        cos_half, sin_half = rope_tables(my_pos)
        cos_tab = jnp.concatenate([cos_half, cos_half], axis=1)
        sin_tab = jnp.concatenate([-sin_half, sin_half], axis=1)
        pos_rows = jnp.broadcast_to(my_pos[:, None, None], (n_seq, 1, slots2))
        dims = (layers, n_y, n_x, rows, depth, q_cols, kv_cols, ffn)
        cols_qkv = q_cols + 2 * kv_cols
        vmem = pl.BlockSpec(memory_space=pltpu.VMEM)
        hbm = pl.BlockSpec(memory_space=pl.ANY)
        cache_shape = (layers, n_seq, slots2, HEAD_DIM)
        norms = 2 * layers
        new_hidden, k_new, v_new = pl.pallas_call(
            functools.partial(step_kernel, dims),
            out_shape=(jax.ShapeDtypeStruct((n_y, rows, depth), BF16), jax.ShapeDtypeStruct(cache_shape, BF16), jax.ShapeDtypeStruct(cache_shape, BF16)),
            in_specs=[vmem] * 8 + [hbm] * 9,
            out_specs=(vmem, hbm, hbm),
            scratch_shapes=[
                pltpu.VMEM((depth, cols_qkv), BF16),
                pltpu.VMEM((q_cols, depth), BF16),
                pltpu.VMEM((depth, ffn), BF16),
                pltpu.VMEM((depth, ffn), BF16),
                pltpu.VMEM((ffn, depth), BF16),
                pltpu.VMEM(cache_shape, BF16),
                pltpu.VMEM(cache_shape, BF16),
                pltpu.VMEM((batch, depth), BF16),
                pltpu.VMEM((norms, n_y * n_x, 1, HEAD_DIM), F32),
                pltpu.VMEM((layers, n_x, n_seq, cols_qkv), BF16),
                pltpu.VMEM((layers, n_x, n_seq, cols_qkv), BF16),
                pltpu.VMEM((16 * n_seq, HEAD_DIM), F32),
                pltpu.VMEM((16 * n_seq, HEAD_DIM), F32),
                pltpu.VMEM((layers, n_x, n_seq, q_cols), BF16),
                pltpu.VMEM((norms, n_y, rows, depth), BF16),
                pltpu.VMEM((norms, n_y, rows, depth), BF16),
                pltpu.VMEM((norms, n_y, rows, depth), BF16),
                pltpu.VMEM((layers, 2, 2, 2, rows, ffn), BF16),
                pltpu.VMEM((layers, 2, 2, rows, ffn), BF16),
                pltpu.VMEM((layers, 2, rows, ffn), BF16),
                pltpu.VMEM((layers, 2, rows, ffn), BF16),
                pltpu.VMEM((layers, n_x, rows, ffn), BF16),
                pltpu.VMEM((batch, depth), F32),
                pltpu.SemaphoreType.DMA((N_REMOTE,)),
                pltpu.SemaphoreType.DMA((N_REMOTE,)),
                pltpu.SemaphoreType.DMA((N_LOCAL,)),
            ],
            compiler_params=pltpu.CompilerParams(collective_id=0, has_side_effects=True, vmem_limit_bytes=64 * 1024 * 1024 - 65536),
        )(hidden.reshape(n_y, rows, depth), pos_rows, cos_tab, sin_tab, g_attn, g_mlp, q_gain, k_gain,
          k_cache.reshape(cache_shape), v_cache.reshape(cache_shape), w_q, w_k, w_v, w_o, w_gate, w_up, w_down)
        return new_hidden.reshape(batch, depth), k_new.reshape(k_cache.shape), v_new.reshape(v_cache.shape)

    return jax.shard_map(device_step, mesh=mesh, in_specs=in_specs, out_specs=out_specs, check_vma=False)
```

time: 397 us -> 139 us (0.35)
  waiting for transfers between devices: 237 us -> 0 us
  Pallas kernels: 0 us -> 128 us
  matrix products: 60.9 us -> 0 us
  other arithmetic: 43.5 us -> 1.54 us
  blocking collectives: 36.6 us -> 0 us
  between operations: 14.6 us -> 0.65 us
  local copies, waits for them, and re-layouts: 2.09 us -> 9.16 us
    psum x6 -> x0, waiting for transfers between devices: 197 us -> none  [the longest x2 69.4 us: device_step(): lax.psum(jnp.dot(attn_all, w_o[layer_idx], preferred_element_type=jnp.flo...]
    pallas_call x0 -> x1, Pallas kernels: none -> 128 us  [device_step(): pl.pallas_call(functools.partial(step_kernel, dims), out_shape=(jax.Shape...]
    dot_general x18 -> x0, matrix products: 60.9 us -> none  [the longest x2 14.5 us: device_step(): jnp.dot(act_val, w_down[layer_idx], preferred_element_type=jnp.float32)]
    reduce_scatter x2 -> x0, waiting for transfers between devices: 39.9 us -> none  [device_step(): lax.psum_scatter(proj_parts, 'x', scatter_dimension=0, tiled=True)]
    psum x4 -> x0, blocking collectives: 25.4 us -> none  [sharded_rms(): lax.psum(jnp.sum(hidden_f32 * hidden_f32, axis=1, keepdims=True), 'x')]
    select_n x3 -> x0, other arithmetic: 18.8 us -> none  [the longest x2 11 us: cache_attention(): k_new = jnp.where(slot_hit, k_rot[:, None], k_cache)]
    all_gather x2 -> x0, blocking collectives: 11.2 us -> none  [device_step(): attn_all = lax.all_gather(attn_local, 'x', axis=0, tiled=True)]
    another operation x5 -> x0, other arithmetic: 8.57 us -> none  [the longest x1 8.17 us: device_step(): return (hidden, jnp.stack(k_list), jnp.stack(v_list))]
  transfers between devices with their start and end apart: 8 -> 0, of which waited for: 8 -> 0; matrix products, arithmetic and copies ran while one was open for 4% -> 0% of each run, Pallas kernels for 0% -> 0%
where the time goes in v1:
time: 139 us
  Pallas kernels  128 us (92%)
  local copies, waits for them, and re-layouts  9.16 us (7%)
  other arithmetic  1.54 us (1%)
    pallas_call x1, Pallas kernels, device_step(): pl.pallas_call(functools.partial(step_kernel, dims), out_shape=(jax.Shape...  128 us
    unnamed x5, local copies, waits for them, and re-layouts  8.47 us

profile of v1, /device:TPU:0, one launch (start us, length us, event | category | flops | bytes accessed | tf_op | source)
XLA Modules:
  0.0 139.2 jit_solution(16474958962796345457)
XLA Ops:
  0.6 0.7 fusion.1
  1.4 0.7 broadcast_in_dim.2.refs_1_
  2.1 0.1 fusion
  2.2 0.7 pad_maximum_fusion
  2.9 127.8 %shard_map.166 = (bf16[4,16,1280]{2,1,0:T(8,128)(2,1)}, bf16[2,16,256,128]{3,2,1,0:T(8,128)(2,1)}, bf16[2,16,256,128]{3,2,1,0:T(8,128)(2,1)}) custom-call(bf16[4,16,1280]{2,1,0:T(8,128)(2,1)} %bitcast.10, s32[16,1,256]{2,1,0:T(1,128)} %broadcast_in_dim.2.refs_1_, f32[16,128]{1,0:T(8,128)} %get-tuple-element.14.refs_2_, f32[16,128]{1,0:T(8,128)} %get-tuple-element.15.refs_3_, ...), custom_call_target="tpu_custom_call" | custom-call | tf_op jit(solution)/shard_map/pallas_call | solution.py:354
  130.7 1.6 %copy.21 = bf16[64,1280]{1,0:T(8,128)(2,1)} copy(bf16[64,1280]{1,0:T(8,128)(2,1)} %bitcast.11) | data formatting | bytes 327680
  132.3 0.0 copy-start
  132.3 5.6 %copy.22 = bf16[2,16,128,2,128]{4,3,2,1,0:T(2,128)(2,1)} copy(bf16[2,16,128,2,128]{4,3,2,1,0:T(2,128)(2,1)} %bitcast.9) | data formatting | bytes 4194304
  137.9 0.0 copy-done
  137.9 1.3 copy.23
  (1 shorter events, 0.0 us)
Async XLA Ops:
  132.3 5.6 %copy-start = (bf16[2,16,256,128]{3,2,1,0:T(8,128)(2,1)S(1)}, bf16[2,16,256,128]{3,2,1,0:T(8,128)(2,1)}, u32[]{:S(2)}) copy-start(bf16[2,16,256,128]{3,2,1,0:T(8,128)(2,1)} %get-tuple-element.8) | copy-start | bytes 6291460

commit v2 on v1

--- a/solution.py
+++ b/solution.py
@@ -2,6 +2,7 @@
 
 import jax
 import jax.numpy as jnp
+import numpy as np
 from jax import lax
 from jax.experimental import pallas as pl
 from jax.experimental.pallas import tpu as pltpu
@@ -19,11 +20,10 @@
 N_LOCAL = 48
 
 
-def rope_tables(positions):
+def inverse_frequencies():
     half_dim = HEAD_DIM // 2
-    inv_freq = jnp.power(ROPE_BASE, -2.0 * jnp.arange(half_dim, dtype=F32) / HEAD_DIM)
-    angles = positions.astype(F32)[:, None] * inv_freq[None, :]
-    return jnp.cos(angles), jnp.sin(angles)
+    freqs = np.power(np.float32(ROPE_BASE), (-2.0 * np.arange(half_dim) / HEAD_DIM).astype(np.float32))
+    return np.concatenate([freqs, freqs])[None].astype(np.float32)
 
 
 def split_tiles(n_tiles, n_chunks):
@@ -34,9 +34,9 @@
 
 def step_kernel(dims, *refs):
     (layers, n_y, n_x, rows, depth, q_cols, kv_cols, ffn) = dims
-    (hid_ref, pos_ref, cos_ref, sin_ref, ga_ref, gm_ref, qg_ref, kg_ref, kc_ref, vc_ref,
+    (hid_ref, pos_ref, freq_ref, ga_ref, gm_ref, qg_ref, kg_ref, kc_ref, vc_ref,
      wq_ref, wk_ref, wv_ref, wo_ref, wg_ref, wu_ref, wd_ref,
-     hid_out, kc_out, vc_out,
+     hid_out, new_out,
      wqkv, wo, wg, wu, wd, kbuf, vbuf, n_buf, stat, qkv_part, qkv_recv, q_rows, o_rows, attn_all,
      ar_part, ar_recv, h_all, gu_part, gu_pair, gu_send, gu_recv, act_all, acc,
      send_sem, recv_sem, local_sem) = refs
@@ -58,7 +58,6 @@
 
     counter = {"remote": 0, "local": 0}
     sent = []
-    stored = []
 
     def remote(src, dst, to_y, to_x):
         i = counter["remote"]
@@ -163,8 +162,14 @@
     for copy in first_stats:
         copy.wait_recv()
 
-    cos_tab = cos_ref[...]
-    sin_tab = sin_ref[...]
+    n_seq = batch // n_x
+    seq_i = lax.broadcasted_iota(jnp.int32, (n_seq, batch), 0)
+    at_lane = lax.broadcasted_iota(jnp.int32, (n_seq, batch), 1)
+    my_pos = jnp.sum(jnp.where(at_lane == seq_i + x * n_seq, pos_ref[...].astype(F32), 0.0), axis=1, keepdims=True)
+    angles = my_pos * freq_ref[...]
+    cos_tab = jnp.cos(angles)
+    sin_tab = jnp.where(lax.broadcasted_iota(jnp.int32, (n_seq, HEAD_DIM), 1) < HEAD_DIM // 2, -1.0, 1.0) * jnp.sin(angles)
+    my_slot = my_pos.astype(jnp.int32)
     slot_row = lax.broadcasted_iota(jnp.int32, (slots2, HEAD_DIM), 0)
     slot_id = slot_row // kv_heads
     head_id = slot_row % kv_heads
@@ -203,16 +208,19 @@
 
         q_gain = qg_ref[...].astype(F32)[layer:layer + 1]
         k_gain = kg_ref[...].astype(F32)[layer:layer + 1]
-        n_seq = batch // n_x
         for h in range(q_heads):
             q_rows[h * n_seq:(h + 1) * n_seq, :] = rotate(proj[:, h * HEAD_DIM:(h + 1) * HEAD_DIM], q_gain)
         k_new = [rotate(proj[:, q_cols + h * HEAD_DIM:q_cols + (h + 1) * HEAD_DIM], k_gain) for h in range(kv_heads)]
         v_new = [proj[:, q_cols + kv_cols + h * HEAD_DIM:q_cols + kv_cols + (h + 1) * HEAD_DIM] for h in range(kv_heads)]
 
+        for h in range(kv_heads):
+            new_out[layer, 0, h] = k_new[h]
+            new_out[layer, 1, h] = v_new[h]
+
         wait_all(pending_cache[layer])
         for b in range(n_seq):
-            pos = pos_ref[b]
-            hit = slot_id == pos[:, :HEAD_DIM]
+            pos = my_slot[b:b + 1]
+            hit = slot_id == pos
             for buf, new in ((kbuf, k_new), (vbuf, v_new)):
                 fresh = new[0][b:b + 1]
                 for h in range(1, kv_heads):
@@ -227,7 +235,6 @@
             e = jnp.exp(scores - top)
             probs = (e / jnp.sum(e, axis=1, keepdims=True)).astype(BF16)
             o_rows[b * 16:(b + 1) * 16, :] = jnp.dot(probs, vbuf[layer, b], preferred_element_type=F32)
-        stored += [local(kbuf.at[layer], kc_out.at[layer]), local(vbuf.at[layer], vc_out.at[layer])]
         for h in range(q_heads):
             attn_all[layer, x, :, h * HEAD_DIM:(h + 1) * HEAD_DIM] = o_rows[pl.ds(h, n_seq, stride=16), :].astype(BF16)
         copies = [remote(attn_all.at[layer, x], attn_all.at[layer, x], y, (x + d) % n_x) for d in (2, 3, 1)]
@@ -323,7 +330,31 @@
     hid_out[...] = residual[...]
     for copy in sent:
         copy.wait_send()
-    wait_all(stored)
+
+
+def cache_kernel(dims, hid_ref, new_ref, pos_ref, kc_ref, vc_ref, hid_out, kc_out, vc_out, hid_buf, kbuf, vbuf, in_sem, out_sem):
+    layers, n_seq, kv_heads = dims
+    first = lax.axis_index("x") * n_seq
+    arrive, leave = [], []
+    for layer in range(layers):
+        for src, dst in ((kc_ref, kbuf), (vc_ref, vbuf)):
+            arrive.append(pltpu.make_async_copy(src.at[layer], dst.at[layer], in_sem.at[len(arrive)]))
+            arrive[-1].start()
+    hidden_in = pltpu.make_async_copy(hid_ref, hid_buf, in_sem.at[len(arrive)])
+    hidden_in.start()
+    for layer in range(layers):
+        for i, (buf, dst) in enumerate(((kbuf, kc_out), (vbuf, vc_out))):
+            arrive[2 * layer + i].wait()
+            for b in range(n_seq):
+                rows = jnp.concatenate([new_ref[layer, i, h, b:b + 1, :] for h in range(kv_heads)], axis=0)
+                buf[layer, b, pos_ref[0, first + b]] = rows.astype(BF16)
+            leave.append(pltpu.make_async_copy(buf.at[layer], dst.at[layer], out_sem.at[len(leave)]))
+            leave[-1].start()
+    hidden_in.wait()
+    leave.append(pltpu.make_async_copy(hid_buf, hid_out, out_sem.at[len(leave)]))
+    leave[-1].start()
+    for copy in leave:
+        copy.wait()
 
 
 def solution(mesh):
@@ -340,22 +371,18 @@
         q_cols, kv_cols, ffn = w_q.shape[2], w_k.shape[2], w_gate.shape[2]
         rows = batch // n_y
         slots2 = slots * kv_heads
-        my_pos = lax.dynamic_slice_in_dim(positions, lax.axis_index('x') * n_seq, n_seq)
-        cos_half, sin_half = rope_tables(my_pos)
-        cos_tab = jnp.concatenate([cos_half, cos_half], axis=1)
-        sin_tab = jnp.concatenate([-sin_half, sin_half], axis=1)
-        pos_rows = jnp.broadcast_to(my_pos[:, None, None], (n_seq, 1, slots2))
         dims = (layers, n_y, n_x, rows, depth, q_cols, kv_cols, ffn)
         cols_qkv = q_cols + 2 * kv_cols
         vmem = pl.BlockSpec(memory_space=pltpu.VMEM)
         hbm = pl.BlockSpec(memory_space=pl.ANY)
         cache_shape = (layers, n_seq, slots2, HEAD_DIM)
         norms = 2 * layers
-        new_hidden, k_new, v_new = pl.pallas_call(
+        positions = positions.reshape(1, batch)
+        new_hidden, new_rows = pl.pallas_call(
             functools.partial(step_kernel, dims),
-            out_shape=(jax.ShapeDtypeStruct((n_y, rows, depth), BF16), jax.ShapeDtypeStruct(cache_shape, BF16), jax.ShapeDtypeStruct(cache_shape, BF16)),
-            in_specs=[vmem] * 8 + [hbm] * 9,
-            out_specs=(vmem, hbm, hbm),
+            out_shape=(jax.ShapeDtypeStruct((n_y, rows, depth), BF16), jax.ShapeDtypeStruct((layers, 2, kv_heads, n_seq, HEAD_DIM), F32)),
+            in_specs=[vmem] * 7 + [hbm] * 9,
+            out_specs=(vmem, vmem),
             scratch_shapes=[
                 pltpu.VMEM((depth, cols_qkv), BF16),
                 pltpu.VMEM((q_cols, depth), BF16),
@@ -385,8 +412,21 @@
                 pltpu.SemaphoreType.DMA((N_LOCAL,)),
             ],
             compiler_params=pltpu.CompilerParams(collective_id=0, has_side_effects=True, vmem_limit_bytes=64 * 1024 * 1024 - 65536),
-        )(hidden.reshape(n_y, rows, depth), pos_rows, cos_tab, sin_tab, g_attn, g_mlp, q_gain, k_gain,
+        )(hidden.reshape(n_y, rows, depth), positions, inverse_frequencies(), g_attn, g_mlp, q_gain, k_gain,
           k_cache.reshape(cache_shape), v_cache.reshape(cache_shape), w_q, w_k, w_v, w_o, w_gate, w_up, w_down)
-        return new_hidden.reshape(batch, depth), k_new.reshape(k_cache.shape), v_new.reshape(v_cache.shape)
+        return pl.pallas_call(
+            functools.partial(cache_kernel, (layers, n_seq, kv_heads)),
+            out_shape=tuple(jax.ShapeDtypeStruct(a.shape, a.dtype) for a in (hidden, k_cache, v_cache)),
+            in_specs=[hbm, vmem, pl.BlockSpec(memory_space=pltpu.SMEM), hbm, hbm],
+            out_specs=(hbm, hbm, hbm),
+            scratch_shapes=[
+                pltpu.VMEM(hidden.shape, BF16),
+                pltpu.VMEM(k_cache.shape, BF16),
+                pltpu.VMEM(k_cache.shape, BF16),
+                pltpu.SemaphoreType.DMA((2 * layers + 1,)),
+                pltpu.SemaphoreType.DMA((2 * layers + 1,)),
+            ],
+            compiler_params=pltpu.CompilerParams(vmem_limit_bytes=64 * 1024 * 1024 - 65536),
+        )(new_hidden.reshape(batch, depth), new_rows, positions, k_cache, v_cache)
 
     return jax.shard_map(device_step, mesh=mesh, in_specs=in_specs, out_specs=out_specs, check_vma=False)

time: 139 us -> 133 us (0.957)
  local copies, waits for them, and re-layouts: 9.16 us -> 0 us
  Pallas kernels: 128 us -> 132 us
  other arithmetic: 1.54 us -> 0 us
    unnamed x5 -> x0, local copies, waits for them, and re-layouts: 8.47 us -> none
    pallas_call x0 -> x1, Pallas kernels: none -> 4.23 us  [device_step(): pl.pallas_call(functools.partial(cache_kernel, (layers, n_seq, kv_heads))...]
where the time goes in v2:
time: 133 us
  Pallas kernels  132 us (99%)
    pallas_call x1, Pallas kernels, device_step(): pl.pallas_call(functools.partial(step_kernel, dims), out_shape=(jax.Shape...  128 us
    pallas_call x1, Pallas kernels, device_step(): pl.pallas_call(functools.partial(cache_kernel, (layers, n_seq, kv_heads))...  4.23 us

profile of v2, /device:TPU:0, one launch (start us, length us, event | category | flops | bytes accessed | tf_op | source)
XLA Modules:
  0.0 132.9 jit_solution(2904787172625902001)
XLA Ops:
  0.6 128.0 %shard_map.175 = (bf16[4,16,1280]{2,1,0:T(8,128)(2,1)}, f32[2,2,2,16,128]{4,3,2,1,0:T(8,128)}) custom-call(bf16[4,16,1280]{2,1,0:T(8,128)(2,1)} %bitcast.7, s32[1,64]{1,0:T(1,128)} %bitcast.9, f32[1,128]{1,0:T(1,128)} %constant.2.clone.refs_2_, bf16[2,1280]{1,0:T(2,128)(2,1)} %refs_3_.1, bf16[2,1280]{1,0:T(2,128)(2,1)} %refs_4_.1, bf16[2,128]{1,0:T(2,128)(2,1)} %refs_5_.1, ...), custom_call_target="tpu_custom_call" | custom-call | tf_op jit(solution)/shard_map/pallas_call | solution.py:381
  128.6 4.2 %shard_map.176 = (bf16[64,1280]{1,0:T(8,128)(2,1)}, bf16[2,16,128,2,128]{4,3,2,1,0:T(2,128)(2,1)}, bf16[2,16,128,2,128]{4,3,2,1,0:T(2,128)(2,1)}) custom-call(bf16[64,1280]{1,0:T(8,128)(2,1)} %bitcast.8, f32[2,2,2,16,128]{4,3,2,1,0:T(8,128)} %get-tuple-element.6.new_ref, s32[1,64]{1,0:T(1,128)} %bitcast.10, bf16[2,16,128,2,128]{4,3,2,1,0:T(2,128)(2,1)} %kc_ref.1, ...), custom_call_target="tpu_custom_call" | custom-call | tf_op jit(solution)/shard_map/pallas_call | solution.py:417

commit v3 on v2

--- a/solution.py
+++ b/solution.py
@@ -12,12 +12,13 @@
 NORM_EPS = 1e-6
 ROPE_BASE = 1000000.0
 TILE = 256
-CHUNKS = 4
+CHUNK_TILES = (2, 3, 4, 4, 2, 2)
+DIRECT = 2
 MESH = pl.DeviceIdType.MESH
 F32 = jnp.float32
 BF16 = jnp.bfloat16
-N_REMOTE = 160
-N_LOCAL = 48
+N_REMOTE = 280
+N_LOCAL = 72
 
 
 def inverse_frequencies():
@@ -26,26 +27,27 @@
     return np.concatenate([freqs, freqs])[None].astype(np.float32)
 
 
-def split_tiles(n_tiles, n_chunks):
-    sizes = [n_tiles // n_chunks + (1 if i < n_tiles % n_chunks else 0) for i in range(n_chunks)]
-    starts = [sum(sizes[:i]) for i in range(n_chunks)]
-    return [(s * TILE, z * TILE) for s, z in zip(starts, sizes) if z]
+def split_tiles(n_tiles):
+    share = n_tiles / sum(CHUNK_TILES)
+    edges = [round(share * sum(CHUNK_TILES[:i])) for i in range(len(CHUNK_TILES) + 1)]
+    return [(a * TILE, (b - a) * TILE) for a, b in zip(edges, edges[1:]) if b > a]
 
 
 def step_kernel(dims, *refs):
     (layers, n_y, n_x, rows, depth, q_cols, kv_cols, ffn) = dims
-    (hid_ref, pos_ref, freq_ref, ga_ref, gm_ref, qg_ref, kg_ref, kc_ref, vc_ref,
+    (hid_any, pos_any, freq_any, ga_any, gm_any, qg_any, kg_any, kc_ref, vc_ref,
      wq_ref, wk_ref, wv_ref, wo_ref, wg_ref, wu_ref, wd_ref,
      hid_out, new_out,
      wqkv, wo, wg, wu, wd, kbuf, vbuf, n_buf, stat, qkv_part, qkv_recv, q_rows, o_rows, attn_all,
      ar_part, ar_recv, h_all, gu_part, gu_pair, gu_send, gu_recv, act_all, acc,
+     hid_ref, pos_ref, freq_ref, ga_ref, gm_ref, qg_ref, kg_ref,
      send_sem, recv_sem, local_sem) = refs
     batch = n_y * rows
     cols_qkv = q_cols + 2 * kv_cols
     q_heads = q_cols // HEAD_DIM
     kv_heads = kv_cols // HEAD_DIM
     group = q_heads // kv_heads
-    chunks = split_tiles(ffn // TILE, CHUNKS)
+    chunks = split_tiles(ffn // TILE)
     model_dim = depth * n_x
     slots2 = kbuf.shape[2]
 
@@ -55,6 +57,7 @@
     core = x % 2
     partner = 2 * chip + (1 - core)
     across = 2 * (1 - chip) + core
+    diagonal = 2 * (1 - chip) + (1 - core)
 
     counter = {"remote": 0, "local": 0}
     sent = []
@@ -103,8 +106,8 @@
     row_i = lax.broadcasted_iota(jnp.int32, (rows, HEAD_DIM), 0)
     lane_i = lax.broadcasted_iota(jnp.int32, (rows, HEAD_DIM), 1)
 
-    def pack_rows(vals_f32, first_row):
-        sums = jnp.sum(vals_f32 * vals_f32, axis=1, keepdims=True)
+    def pack_rows(squares, first_row):
+        sums = jnp.sum(squares, axis=1, keepdims=True)
         return jnp.sum(jnp.where(lane_i == row_i + first_row, sums, 0.0), axis=0, keepdims=True)
 
     all_row = lax.broadcasted_iota(jnp.int32, (batch, HEAD_DIM), 0)
@@ -123,45 +126,55 @@
         vals = hidden_ref[...].reshape(batch, depth).astype(F32)
         n_buf[...] = (vals * scales * gain).astype(BF16)
 
-    def all_reduce(i, residual_ref, with_stats):
-        copies = [remote(ar_part.at[i, (y + d) % n_y], ar_recv.at[i, d], (y + d) % n_y, x) for d in (3, 2, 1)]
-        total = ar_part[i, y].astype(F32)
-        for copy in copies:
-            copy.wait_recv()
-        for d in range(1, n_y):
-            total = total + ar_recv[i, d].astype(F32)
-        new = (residual_ref[y].astype(F32) + total.astype(BF16).astype(F32)).astype(BF16)
-        h_all[i, y] = new
-        gathers = [remote(h_all.at[i, y], h_all.at[i, y], (y + d) % n_y, x) for d in (3, 2, 1)]
-        stats = []
+    def all_reduce(i, tile_product, residual_ref, with_stats):
+        n_tiles = depth // TILE
+        scatters, gathers, stats = [], [], []
+        for t in range(n_tiles):
+            cols = pl.ds(t * TILE, TILE)
+            ar_part[i, :, :, cols] = tile_product(cols).astype(BF16).reshape(n_y, rows, TILE)
+            scatters.append([remote(ar_part.at[i, (y + d) % n_y, :, cols], ar_recv.at[i, d, :, cols], (y + d) % n_y, x) for d in (2, 3, 1)])
+        squares = jnp.zeros((rows, TILE), F32)
+        for t in range(n_tiles):
+            cols = pl.ds(t * TILE, TILE)
+            for copy in scatters[t]:
+                copy.wait_recv()
+            total = ar_part[i, y, :, cols].astype(F32)
+            for d in range(1, n_y):
+                total = total + ar_recv[i, d, :, cols].astype(F32)
+            new = (residual_ref[y, :, cols].astype(F32) + total.astype(BF16).astype(F32)).astype(BF16)
+            h_all[i, y, :, cols] = new
+            gathers += [remote(h_all.at[i, y, :, cols], h_all.at[i, y, :, cols], (y + d) % n_y, x) for d in (2, 3, 1)]
+            squares = squares + new.astype(F32) * new.astype(F32)
         if with_stats:
-            stat[i + 1, 0] = pack_rows(new.astype(F32), y * rows)
+            stat[i + 1, 0] = pack_rows(squares, y * rows)
             stats = [remote(stat.at[i + 1, 0], stat.at[i + 1, dy * n_x + dx], (y + dy) % n_y, (x + dx) % n_x)
-                     for dy in (3, 2, 1, 0) for dx in range(n_x) if dy or dx]
+                     for dy in (2, 3, 1, 0) for dx in range(n_x) if dy or dx]
         for copy in gathers + stats:
             copy.wait_recv()
 
-    pending_qkv = load_qkv(0)
     barrier = pltpu.get_barrier_semaphore()
     for dy in range(n_y):
         for dx in range(n_x):
             if dy or dx:
                 pl.semaphore_signal(barrier, inc=1, device_id={"y": (y + dy) % n_y, "x": (x + dx) % n_x}, device_id_type=MESH)
-    own = jnp.zeros((1, HEAD_DIM), F32)
-    for b in range(n_y):
-        own = own + pack_rows(hid_ref[b].astype(F32), b * rows)
-    stat[0, 0] = own
-    pl.semaphore_wait(barrier, n_y * n_x - 1)
-    first_stats = [remote(stat.at[0, 0], stat.at[0, d], y, (x + d) % n_x) for d in range(1, n_x)]
+    small = [local(src, dst) for src, dst in ((hid_any, hid_ref), (ga_any, ga_ref), (gm_any, gm_ref), (qg_any, qg_ref), (kg_any, kg_ref),
+                                              (pos_any, pos_ref), (freq_any, freq_ref))]
+    pending_qkv = load_qkv(0)
+    wait_all(small)
     pending_o = load_o(0)
     pending_cache = [load_cache(0)]
     pending_gu = [load_gate_up(0, j) for j in range(len(chunks))]
     pending_down = [load_down(0, j) for j in range(len(chunks))]
     pending_cache += [load_cache(layer) for layer in range(1, layers)]
+    gain = ga_ref[...].astype(F32)[0:1]
+    own = jnp.zeros((1, HEAD_DIM), F32)
+    for b in range(n_y):
+        vals = hid_ref[b].astype(F32)
+        own = own + pack_rows(vals * vals, b * rows)
+        sums = jnp.sum(vals * vals, axis=1, keepdims=True)
+        n_buf[b * rows:(b + 1) * rows, :] = (vals * lax.rsqrt(sums / depth + NORM_EPS) * gain).astype(BF16)
+    stat[0, 0] = own
     q_rows[...] = jnp.zeros_like(q_rows)
-    for copy in first_stats:
-        copy.wait_recv()
-
     n_seq = batch // n_x
     seq_i = lax.broadcasted_iota(jnp.int32, (n_seq, batch), 0)
     at_lane = lax.broadcasted_iota(jnp.int32, (n_seq, batch), 1)
@@ -180,24 +193,48 @@
     for layer in range(layers):
         more = layer + 1 < layers
         a, m = 2 * layer, 2 * layer + 1
-        normalise(residual, a, n_x if layer == 0 else n_y * n_x, ga_ref, layer)
+        if layer:
+            normalise(residual, a, n_y * n_x, ga_ref, layer)
         wait_all(pending_qkv)
 
-        def qkv_tile(t, carry):
-            cols = pl.ds(pl.multiple_of(t * TILE, TILE), TILE)
-            part = jnp.dot(n_buf[...], wqkv[:, cols], preferred_element_type=F32).astype(BF16)
-            qkv_part[layer, :, :, cols] = part.reshape(n_x, batch // n_x, TILE)
-            return carry
-
-        lax.fori_loop(0, cols_qkv // TILE, qkv_tile, 0)
-        copies = [remote(qkv_part.at[layer, (x + d) % n_x], qkv_recv.at[layer, d], y, (x + d) % n_x) for d in (2, 3, 1)]
+        def qkv_tiles(first, last):
+            def tile(t, carry):
+                cols = pl.ds(pl.multiple_of(t * TILE, TILE), TILE)
+                part = jnp.dot(n_buf[...], wqkv[:, cols], preferred_element_type=F32).astype(BF16)
+                qkv_part[layer, :, :, cols] = part.reshape(n_x, batch // n_x, TILE)
+                return carry
+
+            lax.fori_loop(first, last, tile, 0)
+
+        def qkv_send(first, last):
+            cols = pl.ds(first * TILE, (last - first) * TILE)
+            return [remote(qkv_part.at[layer, (x + d) % n_x, :, cols], qkv_recv.at[layer, d, :, cols], y, (x + d) % n_x) for d in (2, 3, 1)]
+
+        n_tiles = cols_qkv // TILE
+        copies = []
+        if layer:
+            for first, last in ((0, n_tiles // 2), (n_tiles // 2, n_tiles)):
+                qkv_tiles(first, last)
+                copies += qkv_send(first, last)
+        else:
+            qkv_tiles(0, n_tiles)
+            pl.semaphore_wait(barrier, n_y * n_x - 1)
+            copies += [remote(stat.at[0, 0], stat.at[0, d], y, (x + d) % n_x) for d in (2, 3, 1)]
+            copies += qkv_send(0, n_tiles)
         if more:
             pending_qkv = load_qkv(layer + 1)
-        total = qkv_part[layer, x].astype(F32)
         for copy in copies:
             copy.wait_recv()
-        for d in range(1, n_x):
-            total = total + qkv_recv[layer, d].astype(F32)
+        parts = [qkv_part[layer, x].astype(F32)] + [qkv_recv[layer, d].astype(F32) for d in range(1, n_x)]
+        if not layer:
+            seq_lane = lax.broadcasted_iota(jnp.int32, (n_seq, HEAD_DIM), 1)
+            seq_row = lax.broadcasted_iota(jnp.int32, (n_seq, HEAD_DIM), 0) + x * n_seq
+            sums = [jnp.sum(jnp.where(seq_lane == seq_row, stat[0, d], 0.0), axis=1, keepdims=True) for d in range(n_x)]
+            scale = lax.rsqrt(sum(sums) / model_dim + NORM_EPS)
+            parts = [part * jnp.where(scale > 0.0, scale / lax.rsqrt(own_sum / depth + NORM_EPS), 0.0) for part, own_sum in zip(parts, sums)]
+        total = parts[0]
+        for part in parts[1:]:
+            total = total + part
         proj = total.astype(BF16).astype(F32)
 
         def rotate(vals, gain):
@@ -242,19 +279,15 @@
         for copy in copies:
             copy.wait_recv()
 
-        def o_tile(t, carry):
-            cols = pl.ds(pl.multiple_of(t * TILE, TILE), TILE)
-            part = jnp.dot(attn_all[layer].reshape(batch, q_cols), wo[:, cols], preferred_element_type=F32).astype(BF16)
-            ar_part[a, :, :, cols] = part.reshape(n_y, rows, TILE)
-            return carry
-
-        lax.fori_loop(0, depth // TILE, o_tile, 0)
+        def o_product(cols):
+            return jnp.dot(attn_all[layer].reshape(batch, q_cols), wo[:, cols], preferred_element_type=F32)
+
+        all_reduce(a, o_product, residual, True)
         if more:
             pending_o = load_o(layer + 1)
-        all_reduce(a, residual, True)
 
         normalise(h_all.at[a], a + 1, n_y * n_x, gm_ref, layer)
-        to_pair, to_across, own_gather, across_gather, forward = {}, {}, {}, {}, {}
+        to_pair, to_across, own_gather, across_gather, last_gather = {}, {}, {}, {}, {}
 
         def project(j):
             wait_all(pending_gu[j])
@@ -289,42 +322,58 @@
             act_all[layer, x, :, cols] = (jax.nn.silu(gate_up[0]) * gate_up[1]).astype(BF16)
             mine = act_all.at[layer, x, :, cols]
             across_gather[j] = remote(mine, mine, y, across)
+            if j >= len(chunks) - DIRECT:
+                last_gather[j] = remote(mine, mine, y, diagonal)
             own_gather[j] = remote(mine, mine, y, partner)
 
         def pass_on(j):
             cols = pl.ds(*chunks[j])
             across_gather[j].wait_recv()
-            theirs = act_all.at[layer, across, :, cols]
-            forward[j] = remote(theirs, theirs, y, partner)
+            if j < len(chunks) - DIRECT:
+                theirs = act_all.at[layer, across, :, cols]
+                last_gather[j] = remote(theirs, theirs, y, partner)
+
+        def down_product(j, cols):
+            start, width = chunks[j]
+            vals = act_all[layer, :, :, pl.ds(start, width)].reshape(batch, width)
+            part = jnp.dot(vals, wd[pl.ds(start, width), cols], preferred_element_type=F32)
+            return part + acc[:, cols] if j else part
+
+        def arrived(j):
+            own_gather[j].wait_recv()
+            last_gather[j].wait_recv()
+            wait_all(pending_down[j])
 
         def down(j):
-            own_gather[j].wait_recv()
-            forward[j].wait_recv()
-            wait_all(pending_down[j])
-            start, width = chunks[j]
+            arrived(j)
 
             def tile(t, carry):
                 cols = pl.ds(pl.multiple_of(t * TILE, TILE), TILE)
-                vals = act_all[layer, :, :, pl.ds(start, width)].reshape(batch, width)
-                part = jnp.dot(vals, wd[pl.ds(start, width), cols], preferred_element_type=F32)
-                if j:
-                    part = part + acc[:, cols]
-                if j < len(chunks) - 1:
-                    acc[:, cols] = part
-                else:
-                    ar_part[m, :, :, cols] = part.astype(BF16).reshape(n_y, rows, TILE)
+                acc[:, cols] = down_product(j, cols)
                 return carry
 
             lax.fori_loop(0, depth // TILE, tile, 0)
             if more:
                 pending_down[j] = load_down(layer + 1, j)
 
-        phases = (project, cross, activate, pass_on, down)
-        for stage in range(len(chunks) + len(phases) - 1):
-            for lag, phase in enumerate(phases):
-                if 0 <= stage - lag < len(chunks):
-                    phase(stage - lag)
-        all_reduce(m, h_all.at[a], more)
+        last = len(chunks) - 1
+        for j in range(last + 1):
+            project(j)
+            if j >= 2:
+                cross(j - 2)
+        for j in range(max(last - 1, 0), last + 1):
+            cross(j)
+        for j in range(last + 4):
+            if j <= last:
+                activate(j)
+            if 0 <= j - 2 <= last:
+                pass_on(j - 2)
+            if 0 <= j - 3 < last:
+                down(j - 3)
+        arrived(last)
+        all_reduce(m, functools.partial(down_product, last), h_all.at[a], more)
+        if more:
+            pending_down[last] = load_down(layer + 1, last)
         residual = h_all.at[m]
 
     hid_out[...] = residual[...]
@@ -381,7 +430,7 @@
         new_hidden, new_rows = pl.pallas_call(
             functools.partial(step_kernel, dims),
             out_shape=(jax.ShapeDtypeStruct((n_y, rows, depth), BF16), jax.ShapeDtypeStruct((layers, 2, kv_heads, n_seq, HEAD_DIM), F32)),
-            in_specs=[vmem] * 7 + [hbm] * 9,
+            in_specs=[hbm] * 16,
             out_specs=(vmem, vmem),
             scratch_shapes=[
                 pltpu.VMEM((depth, cols_qkv), BF16),
@@ -407,6 +456,13 @@
                 pltpu.VMEM((layers, 2, rows, ffn), BF16),
                 pltpu.VMEM((layers, n_x, rows, ffn), BF16),
                 pltpu.VMEM((batch, depth), F32),
+                pltpu.VMEM((n_y, rows, depth), BF16),
+                pltpu.VMEM((1, batch), jnp.int32),
+                pltpu.VMEM((1, HEAD_DIM), F32),
+                pltpu.VMEM(g_attn.shape, BF16),
+                pltpu.VMEM(g_mlp.shape, BF16),
+                pltpu.VMEM(q_gain.shape, BF16),
+                pltpu.VMEM(k_gain.shape, BF16),
                 pltpu.SemaphoreType.DMA((N_REMOTE,)),
                 pltpu.SemaphoreType.DMA((N_REMOTE,)),
                 pltpu.SemaphoreType.DMA((N_LOCAL,)),

time: 133 us -> 126 us (0.947)
  Pallas kernels: 132 us -> 125 us
    pallas_call x1, Pallas kernels: 128 us -> 121 us  [device_step(): pl.pallas_call(functools.partial(step_kernel, dims), out_shape=(jax.Shape...]
where the time goes in v3:
time: 126 us
  Pallas kernels  125 us (99%)
    pallas_call x1, Pallas kernels, device_step(): pl.pallas_call(functools.partial(step_kernel, dims), out_shape=(jax.Shape...  121 us
    pallas_call x1, Pallas kernels, device_step(): pl.pallas_call(functools.partial(cache_kernel, (layers, n_seq, kv_heads))...  4.23 us

profile of v3, /device:TPU:0, one launch (start us, length us, event | category | flops | bytes accessed | tf_op | source)
XLA Modules:
  0.0 126.0 jit_solution(10362522557671547891)
XLA Ops:
  0.6 121.1 %shard_map.175 = (bf16[4,16,1280]{2,1,0:T(8,128)(2,1)}, f32[2,2,2,16,128]{4,3,2,1,0:T(8,128)}) custom-call(bf16[4,16,1280]{2,1,0:T(8,128)(2,1)} %bitcast.7, s32[1,64]{1,0:T(1,128)} %bitcast.9, f32[1,128]{1,0:T(1,128)} %constant.2.clone.refs_2_, bf16[2,1280]{1,0:T(2,128)(2,1)} %refs_3_.1, bf16[2,1280]{1,0:T(2,128)(2,1)} %refs_4_.1, bf16[2,128]{1,0:T(2,128)(2,1)} %refs_5_.1, ...), custom_call_target="tpu_custom_call" | custom-call | tf_op jit(solution)/shard_map/pallas_call | solution.py:430
  121.8 4.2 %shard_map.176 = (bf16[64,1280]{1,0:T(8,128)(2,1)}, bf16[2,16,128,2,128]{4,3,2,1,0:T(2,128)(2,1)}, bf16[2,16,128,2,128]{4,3,2,1,0:T(2,128)(2,1)}) custom-call(bf16[64,1280]{1,0:T(8,128)(2,1)} %bitcast.8, f32[2,2,2,16,128]{4,3,2,1,0:T(8,128)} %get-tuple-element.6.new_ref, s32[1,64]{1,0:T(1,128)} %bitcast.10, bf16[2,16,128,2,128]{4,3,2,1,0:T(2,128)(2,1)} %kc_ref.1, ...), custom_call_target="tpu_custom_call" | custom-call | tf_op jit(solution)/shard_map/pallas_call | solution.py:473

commit v4 on v0

v4 whole, which is shorter than its diff:
```python
import functools

import jax
import jax.numpy as jnp
import numpy as np
from jax import lax
from jax.experimental import pallas as pl
from jax.experimental.pallas import tpu as pltpu
from jax.sharding import PartitionSpec as P

HEAD_DIM = 128
NORM_EPS = 1e-6
ROPE_BASE = 1000000.0
TILE = 256
PAIR_LAG = 5
SEQS = 4
MESH = pl.DeviceIdType.MESH
F32 = jnp.float32
BF16 = jnp.bfloat16


def inverse_frequencies():
    half_dim = HEAD_DIM // 2
    freqs = np.power(np.float32(ROPE_BASE), (-2.0 * np.arange(half_dim) / HEAD_DIM).astype(np.float32))
    return np.concatenate([freqs, freqs])[None].astype(np.float32)


def step_kernel(dims, *refs):
    (layers, n_y, n_x, rows, depth, q_cols, kv_cols, ffn) = dims
    (hid_any, pos_any, freq_any, ga_any, gm_any, qg_any, kg_any, kc_ref, vc_ref,
     wq_ref, wk_ref, wv_ref, wo_ref, wg_ref, wu_ref, wd_ref,
     hid_out, new_out,
     wqkv, wo, wg, wu, wd, kbuf, vbuf, n_buf, stat, qkv_part, qkv_recv, q_rows, o_rows, attn_all,
     ar_part, ar_recv, h_mid, h_end, gu_part, gu_pair, gu_send, gu_recv, act_all, acc,
     pos_ref, freq_ref, ga_raw, gm_raw, qg_raw, kg_raw, ga_ref, gm_ref, qg_ref, kg_ref, slot_ref, part_scale, kv_rows,
     send_sem, recv_sem, local_sem) = refs
    batch = n_y * rows
    cols_qkv = q_cols + 2 * kv_cols
    q_heads = q_cols // HEAD_DIM
    kv_heads = kv_cols // HEAD_DIM
    group = q_heads // kv_heads
    model_dim = depth * n_x
    slots2 = kbuf.shape[2]
    n_seq = batch // n_x
    peers = n_y * n_x
    d_tiles, f_tiles, qkv_tiles = depth // TILE, ffn // TILE, cols_qkv // TILE

    y = lax.axis_index("y")
    x = lax.axis_index("x")
    chip = x // 2
    core = x % 2
    partner = 2 * chip + (1 - core)
    across = 2 * (1 - chip) + core
    diagonal = 2 * (1 - chip) + (1 - core)

    at_qkv, at_first, at_attn, at_mid = 0, n_x - 1, 2 * (n_x - 1), 3 * (n_x - 1)
    per_reduce = 2 * (n_y - 1) * d_tiles + peers - 1
    at_end = at_mid + per_reduce
    at_mlp = at_end + per_reduce

    def remote(src, dst, i, to_y, to_x):
        return pltpu.make_async_remote_copy(
            src_ref=src, dst_ref=dst, send_sem=send_sem.at[i], recv_sem=recv_sem.at[i],
            device_id={"y": to_y, "x": to_x}, device_id_type=MESH)

    def each(first, last, body):
        def step(i, carry):
            body(i)
            return carry

        lax.fori_loop(first, last, step, 0)

    def tile_cols(t):
        return pl.ds(pl.multiple_of(t * TILE, TILE), TILE)

    def qkv_loads(layer):
        return [pltpu.make_async_copy(wq_ref.at[layer], wqkv.at[:, 0:q_cols], local_sem.at[0]),
                pltpu.make_async_copy(wk_ref.at[layer], wqkv.at[:, q_cols:q_cols + kv_cols], local_sem.at[1]),
                pltpu.make_async_copy(wv_ref.at[layer], wqkv.at[:, q_cols + kv_cols:cols_qkv], local_sem.at[2])]

    def o_loads(layer):
        return [pltpu.make_async_copy(wo_ref.at[layer], wo, local_sem.at[3])]

    def gate_up_loads(layer):
        half = depth // 2
        return [pltpu.make_async_copy(src.at[layer, r * half:(r + 1) * half, :], dst.at[r * half:(r + 1) * half, :], local_sem.at[4 + 2 * i + r])
                for r in range(2) for i, (src, dst) in enumerate(((wg_ref, wg), (wu_ref, wu)))]

    def down_loads(layer):
        half = ffn // 2
        return [pltpu.make_async_copy(wd_ref.at[layer, r * half:(r + 1) * half, :], wd.at[r * half:(r + 1) * half, :], local_sem.at[8 + r]) for r in range(2)]

    def cache_loads(layer):
        return [pltpu.make_async_copy(src.at[layer], dst.at[layer], local_sem.at[10 + i * layers + layer])
                for i, (src, dst) in enumerate(((kc_ref, kbuf), (vc_ref, vbuf)))]

    def start(copies):
        for copy in copies:
            copy.start()

    def finish(copies):
        for copy in copies:
            copy.wait()

    row_i = lax.broadcasted_iota(jnp.int32, (rows, HEAD_DIM), 0)
    lane_i = lax.broadcasted_iota(jnp.int32, (rows, HEAD_DIM), 1)

    def along_lanes(column, first_row):
        return jnp.sum(jnp.where(lane_i == row_i + first_row, column, 0.0), axis=0, keepdims=True)

    def along_rows(lanes, first_row):
        return jnp.sum(jnp.where(lane_i == row_i + first_row, lanes, 0.0), axis=1, keepdims=True)

    def normalise(hidden_ref, i, gain_ref, layer):
        total = jnp.sum(stat[i], axis=0)
        scales = lax.rsqrt(total / model_dim + NORM_EPS)
        gain = gain_ref[layer]

        def block(b):
            n_buf[pl.ds(pl.multiple_of(b * rows, rows), rows), :] = (hidden_ref[b].astype(F32) * along_rows(scales, b * rows) * gain).astype(BF16)

        each(0, n_y, block)

    def all_reduce(i, base, tile_product, residual_ref, result_ref, with_stats):
        def scatter(t, d):
            cols = tile_cols(t)
            return remote(ar_part.at[i, (y + d) % n_y, :, cols], ar_recv.at[i, d, :, cols], base + t * (n_y - 1) + d - 1, (y + d) % n_y, x)

        def gather(t, d):
            mine = result_ref.at[y, :, tile_cols(t)]
            return remote(mine, mine, base + (d_tiles + t) * (n_y - 1) + d - 1, (y + d) % n_y, x)

        def share(e):
            return remote(stat.at[i + 1, 0], stat.at[i + 1, e], base + 2 * d_tiles * (n_y - 1) + e - 1, (y + e // n_x) % n_y, (x + e % n_x) % n_x)

        def send_tile(t):
            ar_part[i, :, :, tile_cols(t)] = tile_product(tile_cols(t)).astype(BF16).reshape(n_y, rows, TILE)
            for d in (2, 3, 1):
                scatter(t, d).start()

        each(0, d_tiles, send_tile)

        def sum_tile(t, squares):
            cols = tile_cols(t)
            for d in range(1, n_y):
                scatter(t, d).wait_recv()
            total = ar_part[i, y, :, cols].astype(F32)
            for d in range(1, n_y):
                total = total + ar_recv[i, d, :, cols].astype(F32)
            new = (residual_ref[y, :, cols].astype(F32) + total.astype(BF16).astype(F32)).astype(BF16)
            result_ref[y, :, cols] = new
            for d in (2, 3, 1):
                gather(t, d).start()
            return squares + new.astype(F32) * new.astype(F32)

        squares = lax.fori_loop(0, d_tiles, sum_tile, jnp.zeros((rows, TILE), F32))

        def statistics(act):
            @pl.when(with_stats)
            def _():
                each(1, peers, act)

        stat[i + 1, 0] = along_lanes(jnp.sum(squares, axis=1, keepdims=True), y * rows)
        statistics(lambda e: share(e).start())

        def settle(t):
            for d in range(1, n_y):
                gather(t, d).wait_recv()
                scatter(t, d).wait_send()

        each(0, d_tiles, settle)
        statistics(lambda e: share(e).wait_recv())

        def drain():
            def tile(t):
                for d in range(1, n_y):
                    gather(t, d).wait_send()

            each(0, d_tiles, tile)
            statistics(lambda e: share(e).wait_send())

        return drain

    def qkv_copy(d):
        return remote(qkv_part.at[(x + d) % n_x], qkv_recv.at[d], at_qkv + d - 1, y, (x + d) % n_x)

    def first_copy(d):
        return remote(stat.at[0, 0], stat.at[0, d], at_first + d - 1, y, (x + d) % n_x)

    def attn_copy(d):
        return remote(attn_all.at[x], attn_all.at[x], at_attn + d - 1, y, (x + d) % n_x)

    def pair_copy(t):
        cols = tile_cols(t)
        return remote(gu_part.at[:, :, 1 - core, :, cols], gu_pair.at[:, :, :, cols], at_mlp + t, y, partner)

    def across_copy(t):
        cols = tile_cols(t)
        return remote(gu_send.at[:, :, cols], gu_recv.at[:, :, cols], at_mlp + f_tiles + t, y, across)

    def act_copies(t):
        mine = act_all.at[x, :, tile_cols(t)]
        return [remote(mine, mine, at_mlp + (2 + i) * f_tiles + t, y, to_x) for i, to_x in enumerate((diagonal, across, partner))]

    def project_qkv():
        def tile(t):
            cols = tile_cols(t)
            part = jnp.dot(n_buf[...], wqkv[:, cols], preferred_element_type=F32).astype(BF16)
            qkv_part[:, :, cols] = part.reshape(n_x, n_seq, TILE)

        each(0, qkv_tiles, tile)

    barrier = pltpu.get_barrier_semaphore()
    each(1, peers, lambda e: pl.semaphore_signal(
        barrier, inc=1, device_id={"y": (y + e // n_x) % n_y, "x": (x + e % n_x) % n_x}, device_id_type=MESH))
    small = [pltpu.make_async_copy(src, dst, local_sem.at[10 + 2 * layers + i]) for i, (src, dst) in enumerate((
        (hid_any, h_end), (ga_any, ga_raw), (gm_any, gm_raw), (qg_any, qg_raw), (kg_any, kg_raw), (pos_any, pos_ref), (freq_any, freq_ref)))]
    start(small)
    start(qkv_loads(0))
    finish(small)
    start(o_loads(0) + cache_loads(0) + gate_up_loads(0) + down_loads(0))
    for layer in range(1, layers):
        start(cache_loads(layer))
    for raw, wide in ((ga_raw, ga_ref), (gm_raw, gm_ref), (qg_raw, qg_ref), (kg_raw, kg_ref)):
        for layer in range(layers):
            wide[layer] = raw[...].astype(F32)[layer:layer + 1]

    def first_norm(b, lanes):
        vals = h_end[b].astype(F32)
        sums = jnp.sum(vals * vals, axis=1, keepdims=True)
        n_buf[pl.ds(pl.multiple_of(b * rows, rows), rows), :] = (vals * lax.rsqrt(sums / depth + NORM_EPS) * ga_ref[0]).astype(BF16)
        return lanes + along_lanes(sums, b * rows)

    stat[0, 0] = lax.fori_loop(0, n_y, first_norm, jnp.zeros((1, HEAD_DIM), F32))
    q_rows[...] = jnp.zeros_like(q_rows)
    finish(qkv_loads(0))
    project_qkv()
    pl.semaphore_wait(barrier, peers - 1)
    for d in (2, 3, 1):
        first_copy(d).start()
        qkv_copy(d).start()

    my_pos = jnp.sum(
        jnp.where(lax.broadcasted_iota(jnp.int32, (n_seq, batch), 1) == lax.broadcasted_iota(jnp.int32, (n_seq, batch), 0) + x * n_seq,
                  pos_ref[...].astype(F32), 0.0), axis=1, keepdims=True)
    angles = my_pos * freq_ref[...]
    cos_tab = jnp.cos(angles)
    sin_tab = jnp.where(lax.broadcasted_iota(jnp.int32, (n_seq, HEAD_DIM), 1) < HEAD_DIM // 2, -1.0, 1.0) * jnp.sin(angles)
    slot_ref[...] = jnp.broadcast_to(my_pos.astype(jnp.int32), (n_seq, slots2)).reshape(slot_ref.shape)

    slot_row = lax.broadcasted_iota(jnp.int32, (slots2, HEAD_DIM), 0)
    slot_id = slot_row // kv_heads
    head_id = slot_row % kv_heads
    score_col = lax.broadcasted_iota(jnp.int32, (16, slots2), 1)
    score_head = lax.broadcasted_iota(jnp.int32, (16, slots2), 0) // group
    score_slot = score_col // kv_heads
    score_own = (score_col % kv_heads == score_head) | (score_head >= kv_heads)

    for d in range(1, n_x):
        first_copy(d).wait_recv()
        first_copy(d).wait_send()
    sums = [along_rows(stat[0, d], x * n_seq) for d in range(n_x)]
    scale = lax.rsqrt(sum(sums) / model_dim + NORM_EPS)
    for d in range(n_x):
        part_scale[d] = jnp.broadcast_to(jnp.where(scale > 0.0, scale / lax.rsqrt(sums[d] / depth + NORM_EPS), 0.0), (n_seq, TILE))

    def run_layer(layer):
        more = layer + 1 < layers

        def reload(loads):
            @pl.when(more)
            def _():
                start(loads(layer + 1))

        reload(qkv_loads)
        for d in range(1, n_x):
            qkv_copy(d).wait_recv()

        def projected(cols, scale_cols):
            total = qkv_part[x, :, cols].astype(F32) * part_scale[0, :, scale_cols]
            for d in range(1, n_x):
                total = total + qkv_recv[d, :, cols].astype(F32) * part_scale[d, :, scale_cols]
            return total.astype(BF16).astype(F32)

        for h in range(q_heads + kv_heads):
            vals = projected(pl.ds(h * HEAD_DIM, HEAD_DIM), pl.ds(0, HEAD_DIM))
            mean_sq = jnp.mean(vals * vals, axis=-1, keepdims=True)
            normed = vals * lax.rsqrt(mean_sq + NORM_EPS) * (qg_ref if h < q_heads else kg_ref)[layer]
            turned = (normed * cos_tab + pltpu.roll(normed, HEAD_DIM // 2, 1) * sin_tab).astype(BF16).astype(F32)
            if h < q_heads:
                q_rows[pl.ds(h, n_seq, stride=16), :] = turned
            else:
                new_out[layer, 0, h - q_heads] = turned
                kv_rows[0, h - q_heads] = turned.reshape(n_seq, 1, HEAD_DIM)
        for h in range(kv_heads):
            vals = projected(pl.ds(q_cols + kv_cols + h * HEAD_DIM, HEAD_DIM), pl.ds(0, HEAD_DIM))
            new_out[layer, 1, h] = vals
            kv_rows[1, h] = vals.reshape(n_seq, 1, HEAD_DIM)

        finish(cache_loads(layer))

        def sequences(i):
            for u in range(SEQS):
                b = i * SEQS + u
                slots = slot_ref[b]
                hit = slot_id == slots[:, :HEAD_DIM]
                for j, buf in enumerate((kbuf, vbuf)):
                    fresh = kv_rows[j, 0, b]
                    for h in range(1, kv_heads):
                        fresh = jnp.where(head_id == h, kv_rows[j, h, b], fresh)
                    buf[layer, b] = jnp.where(hit, fresh, buf[layer, b].astype(F32)).astype(BF16)
                q_b = q_rows[pl.ds(pl.multiple_of(b * 16, 16), 16), :].astype(BF16)
                scores = lax.dot_general(q_b, kbuf[layer, b], (((1,), (1,)), ((), ())), preferred_element_type=F32) * (HEAD_DIM ** -0.5)
                scores = jnp.where(score_own & (score_slot <= slots), scores, -1e30)
                top = jnp.max(scores, axis=1, keepdims=True)
                e = jnp.exp(scores - top)
                probs = (e / jnp.sum(e, axis=1, keepdims=True)).astype(BF16)
                o_rows[pl.ds(pl.multiple_of(b * 16, 16), 16), :] = jnp.dot(probs, vbuf[layer, b], preferred_element_type=F32)

        each(0, n_seq // SEQS, sequences)
        for h in range(q_heads):
            attn_all[x, :, h * HEAD_DIM:(h + 1) * HEAD_DIM] = o_rows[pl.ds(h, n_seq, stride=16), :].astype(BF16)
        for d in (2, 3, 1):
            attn_copy(d).start()
        finish(o_loads(layer))
        for d in range(1, n_x):
            qkv_copy(d).wait_send()
            attn_copy(d).wait_recv()

        drain_mid = all_reduce(
            0, at_mid, lambda cols: jnp.dot(attn_all[...].reshape(batch, q_cols), wo[:, cols], preferred_element_type=F32), h_end, h_mid, True)
        reload(o_loads)

        normalise(h_mid, 1, gm_ref, layer)
        finish(gate_up_loads(layer))

        def project(s):
            @pl.when(s < f_tiles)
            def _():
                cols = tile_cols(s)
                gate = jnp.dot(n_buf[...], wg[:, cols], preferred_element_type=F32).astype(BF16)
                up = jnp.dot(n_buf[...], wu[:, cols], preferred_element_type=F32).astype(BF16)
                gu_part[0, :, :, :, cols] = gate.reshape(2, 2, rows, TILE)
                gu_part[1, :, :, :, cols] = up.reshape(2, 2, rows, TILE)
                pair_copy(s).start()

            @pl.when(s >= PAIR_LAG)
            def _():
                t = s - PAIR_LAG
                cols = tile_cols(t)
                pair_copy(t).wait_recv()
                pair = gu_part[:, 1 - chip, core, :, cols].astype(F32) + gu_pair[:, 1 - chip, :, cols].astype(F32)
                gu_send[:, :, cols] = pair.astype(BF16)
                across_copy(t).start()

        each(0, f_tiles + PAIR_LAG, project)
        reload(gate_up_loads)

        def activate(t):
            cols = tile_cols(t)
            across_copy(t).wait_recv()
            gate_up = (gu_part[:, chip, core, :, cols].astype(F32) + gu_pair[:, chip, :, cols].astype(F32)
                       + gu_recv[:, :, cols].astype(F32)).astype(BF16).astype(F32)
            act_all[x, :, cols] = (jax.nn.silu(gate_up[0]) * gate_up[1]).astype(BF16)
            start(act_copies(t))

        each(0, f_tiles, activate)
        drain_mid()
        for d in range(1, n_x):
            attn_copy(d).wait_send()
        acc[...] = jnp.zeros_like(acc)
        finish(down_loads(layer))

        def down(t):
            for copy in act_copies(t):
                copy.wait_recv()
            vals = act_all[:, :, tile_cols(t)].reshape(batch, TILE)
            acc[...] += jnp.dot(vals, wd[tile_cols(t), :], preferred_element_type=F32)

        each(0, f_tiles, down)
        reload(down_loads)
        drain_end = all_reduce(1, at_end, lambda cols: acc[:, cols], h_mid, h_end, more)

        @pl.when(more)
        def _():
            normalise(h_end, 2, ga_ref, layer + 1)
            part_scale[...] = jnp.ones_like(part_scale)
            finish(qkv_loads(layer + 1))
            project_qkv()
            for d in (2, 3, 1):
                qkv_copy(d).start()

        drain_end()

        def drain_mlp(t):
            pair_copy(t).wait_send()
            across_copy(t).wait_send()
            for copy in act_copies(t):
                copy.wait_send()

        each(0, f_tiles, drain_mlp)

    each(0, layers, run_layer)
    hid_out[...] = h_end[...]


def cache_kernel(dims, hid_ref, new_ref, pos_ref, kc_ref, vc_ref, hid_out, kc_out, vc_out, hid_buf, kbuf, vbuf, in_sem, out_sem):
    layers, n_seq, kv_heads = dims
    first = lax.axis_index("x") * n_seq
    arrive, leave = [], []
    for layer in range(layers):
        for src, dst in ((kc_ref, kbuf), (vc_ref, vbuf)):
            arrive.append(pltpu.make_async_copy(src.at[layer], dst.at[layer], in_sem.at[len(arrive)]))
            arrive[-1].start()
    hidden_in = pltpu.make_async_copy(hid_ref, hid_buf, in_sem.at[len(arrive)])
    hidden_in.start()
    for layer in range(layers):
        for i, (buf, dst) in enumerate(((kbuf, kc_out), (vbuf, vc_out))):
            arrive[2 * layer + i].wait()
            for b in range(n_seq):
                rows = jnp.concatenate([new_ref[layer, i, h, b:b + 1, :] for h in range(kv_heads)], axis=0)
                buf[layer, b, pos_ref[0, first + b]] = rows.astype(BF16)
            leave.append(pltpu.make_async_copy(buf.at[layer], dst.at[layer], out_sem.at[len(leave)]))
            leave[-1].start()
    hidden_in.wait()
    leave.append(pltpu.make_async_copy(hid_buf, hid_out, out_sem.at[len(leave)]))
    leave[-1].start()
    for copy in leave:
        copy.wait()


def solution(mesh):
    n_x, n_y = mesh.shape['x'], mesh.shape['y']
    cache_spec = P(None, ('dp', 'x'), None, 'y', None)
    col_spec = P(None, 'x', 'y')
    row_spec = P(None, 'y', 'x')
    in_specs = (P('dp', 'x'), P('dp'), cache_spec, cache_spec, P(None, 'x'), P(None, 'x'), P(), P(), col_spec, col_spec, col_spec, row_spec, col_spec, col_spec, row_spec)
    out_specs = (P('dp', 'x'), cache_spec, cache_spec)

    def device_step(hidden, positions, k_cache, v_cache, g_attn, g_mlp, q_gain, k_gain, w_q, w_k, w_v, w_o, w_gate, w_up, w_down):
        batch, depth = hidden.shape
        layers, n_seq, slots, kv_heads, _ = k_cache.shape
        q_cols, kv_cols, ffn = w_q.shape[2], w_k.shape[2], w_gate.shape[2]
        rows = batch // n_y
        slots2 = slots * kv_heads
        dims = (layers, n_y, n_x, rows, depth, q_cols, kv_cols, ffn)
        cols_qkv = q_cols + 2 * kv_cols
        vmem = pl.BlockSpec(memory_space=pltpu.VMEM)
        hbm = pl.BlockSpec(memory_space=pl.ANY)
        cache_shape = (layers, n_seq, slots2, HEAD_DIM)
        peers = n_y * n_x
        d_tiles, f_tiles = depth // TILE, ffn // TILE
        copies = 3 * (n_x - 1) + 2 * (2 * (n_y - 1) * d_tiles + peers - 1) + 5 * f_tiles
        positions = positions.reshape(1, batch)
        new_hidden, new_rows = pl.pallas_call(
            functools.partial(step_kernel, dims),
            out_shape=(jax.ShapeDtypeStruct((n_y, rows, depth), BF16), jax.ShapeDtypeStruct((layers, 2, kv_heads, n_seq, HEAD_DIM), F32)),
            in_specs=[hbm] * 16,
            out_specs=(vmem, vmem),
            scratch_shapes=[
                pltpu.VMEM((depth, cols_qkv), BF16),
                pltpu.VMEM((q_cols, depth), BF16),
                pltpu.VMEM((depth, ffn), BF16),
                pltpu.VMEM((depth, ffn), BF16),
                pltpu.VMEM((ffn, depth), BF16),
                pltpu.VMEM(cache_shape, BF16),
                pltpu.VMEM(cache_shape, BF16),
                pltpu.VMEM((batch, depth), BF16),
                pltpu.VMEM((3, peers, 1, HEAD_DIM), F32),
                pltpu.VMEM((n_x, n_seq, cols_qkv), BF16),
                pltpu.VMEM((n_x, n_seq, cols_qkv), BF16),
                pltpu.VMEM((16 * n_seq, HEAD_DIM), F32),
                pltpu.VMEM((16 * n_seq, HEAD_DIM), F32),
                pltpu.VMEM((n_x, n_seq, q_cols), BF16),
                pltpu.VMEM((2, n_y, rows, depth), BF16),
                pltpu.VMEM((2, n_y, rows, depth), BF16),
                pltpu.VMEM((n_y, rows, depth), BF16),
                pltpu.VMEM((n_y, rows, depth), BF16),
                pltpu.VMEM((2, 2, 2, rows, ffn), BF16),
                pltpu.VMEM((2, 2, rows, ffn), BF16),
                pltpu.VMEM((2, rows, ffn), BF16),
                pltpu.VMEM((2, rows, ffn), BF16),
                pltpu.VMEM((n_x, rows, ffn), BF16),
                pltpu.VMEM((batch, depth), F32),
                pltpu.VMEM((1, batch), jnp.int32),
                pltpu.VMEM((1, HEAD_DIM), F32),
                pltpu.VMEM(g_attn.shape, BF16),
                pltpu.VMEM(g_mlp.shape, BF16),
                pltpu.VMEM(q_gain.shape, BF16),
                pltpu.VMEM(k_gain.shape, BF16),
                pltpu.VMEM((layers, 1, depth), F32),
                pltpu.VMEM((layers, 1, depth), F32),
                pltpu.VMEM((layers, 1, HEAD_DIM), F32),
                pltpu.VMEM((layers, 1, HEAD_DIM), F32),
                pltpu.VMEM((n_seq, 1, slots2), jnp.int32),
                pltpu.VMEM((n_x, n_seq, TILE), F32),
                pltpu.VMEM((2, kv_heads, n_seq, 1, HEAD_DIM), F32),
                pltpu.SemaphoreType.DMA((copies,)),
                pltpu.SemaphoreType.DMA((copies,)),
                pltpu.SemaphoreType.DMA((17 + 2 * layers,)),
            ],
            compiler_params=pltpu.CompilerParams(collective_id=0, has_side_effects=True, vmem_limit_bytes=64 * 1024 * 1024 - 65536),
        )(hidden.reshape(n_y, rows, depth), positions, inverse_frequencies(), g_attn, g_mlp, q_gain, k_gain,
          k_cache.reshape(cache_shape), v_cache.reshape(cache_shape), w_q, w_k, w_v, w_o, w_gate, w_up, w_down)
        return pl.pallas_call(
            functools.partial(cache_kernel, (layers, n_seq, kv_heads)),
            out_shape=tuple(jax.ShapeDtypeStruct(a.shape, a.dtype) for a in (hidden, k_cache, v_cache)),
            in_specs=[hbm, vmem, pl.BlockSpec(memory_space=pltpu.SMEM), hbm, hbm],
            out_specs=(hbm, hbm, hbm),
            scratch_shapes=[
                pltpu.VMEM(hidden.shape, BF16),
                pltpu.VMEM(k_cache.shape, BF16),
                pltpu.VMEM(k_cache.shape, BF16),
                pltpu.SemaphoreType.DMA((2 * layers + 1,)),
                pltpu.SemaphoreType.DMA((2 * layers + 1,)),
            ],
            compiler_params=pltpu.CompilerParams(vmem_limit_bytes=64 * 1024 * 1024 - 65536),
        )(new_hidden.reshape(batch, depth), new_rows, positions, k_cache, v_cache)

    return jax.shard_map(device_step, mesh=mesh, in_specs=in_specs, out_specs=out_specs, check_vma=False)
```

time: 397 us -> 121 us (0.30)
  waiting for transfers between devices: 237 us -> 0 us
  Pallas kernels: 0 us -> 120 us
  matrix products: 60.9 us -> 0 us
  other arithmetic: 43.5 us -> 0 us
  blocking collectives: 36.6 us -> 0 us
  between operations: 14.6 us -> 0.64 us
    psum x6 -> x0, waiting for transfers between devices: 197 us -> none  [the longest x2 69.4 us: device_step(): lax.psum(jnp.dot(attn_all, w_o[layer_idx], preferred_element_type=jnp.flo...]
    pallas_call x0 -> x2, Pallas kernels: none -> 120 us  [the longest x1 116 us: device_step(): pl.pallas_call(functools.partial(step_kernel, dims), out_shape=(jax.Shape...]
    dot_general x18 -> x0, matrix products: 60.9 us -> none  [the longest x2 14.5 us: device_step(): jnp.dot(act_val, w_down[layer_idx], preferred_element_type=jnp.float32)]
    reduce_scatter x2 -> x0, waiting for transfers between devices: 39.9 us -> none  [device_step(): lax.psum_scatter(proj_parts, 'x', scatter_dimension=0, tiled=True)]
    psum x4 -> x0, blocking collectives: 25.4 us -> none  [sharded_rms(): lax.psum(jnp.sum(hidden_f32 * hidden_f32, axis=1, keepdims=True), 'x')]
    select_n x3 -> x0, other arithmetic: 18.8 us -> none  [the longest x2 11 us: cache_attention(): k_new = jnp.where(slot_hit, k_rot[:, None], k_cache)]
    all_gather x2 -> x0, blocking collectives: 11.2 us -> none  [device_step(): attn_all = lax.all_gather(attn_local, 'x', axis=0, tiled=True)]
    another operation x5 -> x0, other arithmetic: 8.57 us -> none  [the longest x1 8.17 us: device_step(): return (hidden, jnp.stack(k_list), jnp.stack(v_list))]
  transfers between devices with their start and end apart: 8 -> 0, of which waited for: 8 -> 0; matrix products, arithmetic and copies ran while one was open for 4% -> 0% of each run, Pallas kernels for 0% -> 0%
where the time goes in v4:
time: 121 us
  Pallas kernels  120 us (99%)
    pallas_call x1, Pallas kernels, device_step(): pl.pallas_call(functools.partial(step_kernel, dims), out_shape=(jax.Shape...  116 us
    pallas_call x1, Pallas kernels, device_step(): pl.pallas_call(functools.partial(cache_kernel, (layers, n_seq, kv_heads))...  4.23 us

profile of v4, /device:TPU:0, one launch (start us, length us, event | category | flops | bytes accessed | tf_op | source)
XLA Modules:
  0.0 120.9 jit_solution(8388168859306497880)
XLA Ops:
  0.6 116.1 %shard_map.175 = (bf16[4,16,1280]{2,1,0:T(8,128)(2,1)}, f32[2,2,2,16,128]{4,3,2,1,0:T(8,128)}) custom-call(bf16[4,16,1280]{2,1,0:T(8,128)(2,1)} %bitcast.7, s32[1,64]{1,0:T(1,128)} %bitcast.9, f32[1,128]{1,0:T(1,128)} %constant.2.clone.refs_2_, bf16[2,1280]{1,0:T(2,128)(2,1)} %refs_3_.1, bf16[2,1280]{1,0:T(2,128)(2,1)} %refs_4_.1, bf16[2,128]{1,0:T(2,128)(2,1)} %refs_5_.1, ...), custom_call_target="tpu_custom_call" | custom-call | tf_op jit(solution)/shard_map/pallas_call | solution.py:455
  116.7 4.2 %shard_map.176 = (bf16[64,1280]{1,0:T(8,128)(2,1)}, bf16[2,16,128,2,128]{4,3,2,1,0:T(2,128)(2,1)}, bf16[2,16,128,2,128]{4,3,2,1,0:T(2,128)(2,1)}) custom-call(bf16[64,1280]{1,0:T(8,128)(2,1)} %bitcast.8, f32[2,2,2,16,128]{4,3,2,1,0:T(8,128)} %get-tuple-element.6.new_ref, s32[1,64]{1,0:T(1,128)} %bitcast.10, bf16[2,16,128,2,128]{4,3,2,1,0:T(2,128)(2,1)} %kc_ref.1, ...), custom_call_target="tpu_custom_call" | custom-call | tf_op jit(solution)/shard_map/pallas_call | solution.py:505

commit v5 on v4

--- a/solution.py
+++ b/solution.py
@@ -12,7 +12,7 @@
 NORM_EPS = 1e-6
 ROPE_BASE = 1000000.0
 TILE = 256
-PAIR_LAG = 5
+GROUP_TILES = (3, 3, 3, 3, 3, 2)
 SEQS = 4
 MESH = pl.DeviceIdType.MESH
 F32 = jnp.float32
@@ -23,6 +23,12 @@
     half_dim = HEAD_DIM // 2
     freqs = np.power(np.float32(ROPE_BASE), (-2.0 * np.arange(half_dim) / HEAD_DIM).astype(np.float32))
     return np.concatenate([freqs, freqs])[None].astype(np.float32)
+
+
+def split_tiles(n_tiles):
+    share = n_tiles / sum(GROUP_TILES)
+    edges = [round(share * sum(GROUP_TILES[:i])) for i in range(len(GROUP_TILES) + 1)]
+    return [(a, b) for a, b in zip(edges, edges[1:]) if b > a]
 
 
 def step_kernel(dims, *refs):
@@ -32,7 +38,7 @@
      hid_out, new_out,
      wqkv, wo, wg, wu, wd, kbuf, vbuf, n_buf, stat, qkv_part, qkv_recv, q_rows, o_rows, attn_all,
      ar_part, ar_recv, h_mid, h_end, gu_part, gu_pair, gu_send, gu_recv, act_all, acc,
-     pos_ref, freq_ref, ga_raw, gm_raw, qg_raw, kg_raw, ga_ref, gm_ref, qg_ref, kg_ref, slot_ref, part_scale, kv_rows,
+     pos_ref, freq_ref, ga_raw, gm_raw, qg_raw, kg_raw, ga_ref, gm_ref, qg_ref, kg_ref, slot_ref, part_scale, kv_rows, s_rows, p_rows,
      send_sem, recv_sem, local_sem) = refs
     batch = n_y * rows
     cols_qkv = q_cols + 2 * kv_cols
@@ -53,15 +59,21 @@
     across = 2 * (1 - chip) + core
     diagonal = 2 * (1 - chip) + (1 - core)
 
-    at_qkv, at_first, at_attn, at_mid = 0, n_x - 1, 2 * (n_x - 1), 3 * (n_x - 1)
-    per_reduce = 2 * (n_y - 1) * d_tiles + peers - 1
-    at_end = at_mid + per_reduce
-    at_mlp = at_end + per_reduce
-
-    def remote(src, dst, i, to_y, to_x):
+    groups = split_tiles(f_tiles)
+    at_qkv, at_first, at_attn, at_mid = 0, 1, 2, 3
+    at_end = at_mid + d_tiles + 2
+    at_mlp = at_end + d_tiles + 2
+
+    def remote(src, dst, to_send, to_recv, to_y, to_x):
         return pltpu.make_async_remote_copy(
-            src_ref=src, dst_ref=dst, send_sem=send_sem.at[i], recv_sem=recv_sem.at[i],
+            src_ref=src, dst_ref=dst, send_sem=send_sem.at[to_send], recv_sem=recv_sem.at[to_recv],
             device_id={"y": to_y, "x": to_x}, device_id_type=MESH)
+
+    def received(i, like):
+        pltpu.make_async_copy(like, like, recv_sem.at[i]).wait()
+
+    def delivered(i, like):
+        pltpu.make_async_copy(like, like, send_sem.at[i]).wait()
 
     def each(first, last, body):
         def step(i, carry):
@@ -82,16 +94,13 @@
         return [pltpu.make_async_copy(wo_ref.at[layer], wo, local_sem.at[3])]
 
     def gate_up_loads(layer):
-        half = depth // 2
-        return [pltpu.make_async_copy(src.at[layer, r * half:(r + 1) * half, :], dst.at[r * half:(r + 1) * half, :], local_sem.at[4 + 2 * i + r])
-                for r in range(2) for i, (src, dst) in enumerate(((wg_ref, wg), (wu_ref, wu)))]
+        return [pltpu.make_async_copy(src.at[layer], dst, local_sem.at[4 + i]) for i, (src, dst) in enumerate(((wg_ref, wg), (wu_ref, wu)))]
 
     def down_loads(layer):
-        half = ffn // 2
-        return [pltpu.make_async_copy(wd_ref.at[layer, r * half:(r + 1) * half, :], wd.at[r * half:(r + 1) * half, :], local_sem.at[8 + r]) for r in range(2)]
+        return [pltpu.make_async_copy(wd_ref.at[layer], wd, local_sem.at[6])]
 
     def cache_loads(layer):
-        return [pltpu.make_async_copy(src.at[layer], dst.at[layer], local_sem.at[10 + i * layers + layer])
+        return [pltpu.make_async_copy(src.at[layer], dst.at[layer], local_sem.at[7 + i * layers + layer])
                 for i, (src, dst) in enumerate(((kc_ref, kbuf), (vc_ref, vbuf)))]
 
     def start(copies):
@@ -122,16 +131,19 @@
         each(0, n_y, block)
 
     def all_reduce(i, base, tile_product, residual_ref, result_ref, with_stats):
+        others = n_y - 1
+        send = 3 + 3 * i
+
         def scatter(t, d):
             cols = tile_cols(t)
-            return remote(ar_part.at[i, (y + d) % n_y, :, cols], ar_recv.at[i, d, :, cols], base + t * (n_y - 1) + d - 1, (y + d) % n_y, x)
+            return remote(ar_part.at[i, (y + d) % n_y, :, cols], ar_recv.at[i, d, :, cols], send, base + t, (y + d) % n_y, x)
 
         def gather(t, d):
             mine = result_ref.at[y, :, tile_cols(t)]
-            return remote(mine, mine, base + (d_tiles + t) * (n_y - 1) + d - 1, (y + d) % n_y, x)
+            return remote(mine, mine, send + 1, base + d_tiles, (y + d) % n_y, x)
 
         def share(e):
-            return remote(stat.at[i + 1, 0], stat.at[i + 1, e], base + 2 * d_tiles * (n_y - 1) + e - 1, (y + e // n_x) % n_y, (x + e % n_x) % n_x)
+            return remote(stat.at[i + 1, 0], stat.at[i + 1, e], send + 2, base + d_tiles + 1, (y + e // n_x) % n_y, (x + e % n_x) % n_x)
 
         def send_tile(t):
             ar_part[i, :, :, tile_cols(t)] = tile_product(tile_cols(t)).astype(BF16).reshape(n_y, rows, TILE)
@@ -142,8 +154,7 @@
 
         def sum_tile(t, squares):
             cols = tile_cols(t)
-            for d in range(1, n_y):
-                scatter(t, d).wait_recv()
+            received(base + t, ar_recv.at[i, 1:n_y, :, cols])
             total = ar_part[i, y, :, cols].astype(F32)
             for d in range(1, n_y):
                 total = total + ar_recv[i, d, :, cols].astype(F32)
@@ -154,53 +165,51 @@
             return squares + new.astype(F32) * new.astype(F32)
 
         squares = lax.fori_loop(0, d_tiles, sum_tile, jnp.zeros((rows, TILE), F32))
-
-        def statistics(act):
+        stat[i + 1, 0] = along_lanes(jnp.sum(squares, axis=1, keepdims=True), y * rows)
+
+        @pl.when(with_stats)
+        def _():
+            each(1, peers, lambda e: share(e).start())
+
+        received(base + d_tiles, ar_recv.at[i, 1:n_y])
+
+        @pl.when(with_stats)
+        def _():
+            received(base + d_tiles + 1, stat.at[i + 1, 1:peers])
+
+        def drain():
+            delivered(send, ar_recv.at[i, 1:n_y])
+            delivered(send + 1, ar_recv.at[i, 1:n_y])
+
             @pl.when(with_stats)
             def _():
-                each(1, peers, act)
-
-        stat[i + 1, 0] = along_lanes(jnp.sum(squares, axis=1, keepdims=True), y * rows)
-        statistics(lambda e: share(e).start())
-
-        def settle(t):
-            for d in range(1, n_y):
-                gather(t, d).wait_recv()
-                scatter(t, d).wait_send()
-
-        each(0, d_tiles, settle)
-        statistics(lambda e: share(e).wait_recv())
-
-        def drain():
-            def tile(t):
-                for d in range(1, n_y):
-                    gather(t, d).wait_send()
-
-            each(0, d_tiles, tile)
-            statistics(lambda e: share(e).wait_send())
+                delivered(send + 2, stat.at[i + 1, 1:peers])
 
         return drain
 
     def qkv_copy(d):
-        return remote(qkv_part.at[(x + d) % n_x], qkv_recv.at[d], at_qkv + d - 1, y, (x + d) % n_x)
+        return remote(qkv_part.at[(x + d) % n_x], qkv_recv.at[d], 0, at_qkv, y, (x + d) % n_x)
 
     def first_copy(d):
-        return remote(stat.at[0, 0], stat.at[0, d], at_first + d - 1, y, (x + d) % n_x)
+        return remote(stat.at[0, 0], stat.at[0, d], 1, at_first, y, (x + d) % n_x)
 
     def attn_copy(d):
-        return remote(attn_all.at[x], attn_all.at[x], at_attn + d - 1, y, (x + d) % n_x)
-
-    def pair_copy(t):
-        cols = tile_cols(t)
-        return remote(gu_part.at[:, :, 1 - core, :, cols], gu_pair.at[:, :, :, cols], at_mlp + t, y, partner)
-
-    def across_copy(t):
-        cols = tile_cols(t)
-        return remote(gu_send.at[:, :, cols], gu_recv.at[:, :, cols], at_mlp + f_tiles + t, y, across)
-
-    def act_copies(t):
-        mine = act_all.at[x, :, tile_cols(t)]
-        return [remote(mine, mine, at_mlp + (2 + i) * f_tiles + t, y, to_x) for i, to_x in enumerate((diagonal, across, partner))]
+        return remote(attn_all.at[x], attn_all.at[x], 2, at_attn, y, (x + d) % n_x)
+
+    def group_cols(g):
+        return pl.ds(groups[g][0] * TILE, (groups[g][1] - groups[g][0]) * TILE)
+
+    def pair_copy(g):
+        cols = group_cols(g)
+        return remote(gu_part.at[:, :, 1 - core, :, cols], gu_pair.at[:, :, :, cols], 9, at_mlp + g, y, partner)
+
+    def across_copy(g):
+        cols = group_cols(g)
+        return remote(gu_send.at[:, :, cols], gu_recv.at[:, :, cols], 10, at_mlp + len(groups) + g, y, across)
+
+    def act_copies(g):
+        mine = act_all.at[x, :, group_cols(g)]
+        return [remote(mine, mine, 11, at_mlp + 2 * len(groups) + g, y, to_x) for to_x in (diagonal, across, partner)]
 
     def project_qkv():
         def tile(t):
@@ -213,7 +222,7 @@
     barrier = pltpu.get_barrier_semaphore()
     each(1, peers, lambda e: pl.semaphore_signal(
         barrier, inc=1, device_id={"y": (y + e // n_x) % n_y, "x": (x + e % n_x) % n_x}, device_id_type=MESH))
-    small = [pltpu.make_async_copy(src, dst, local_sem.at[10 + 2 * layers + i]) for i, (src, dst) in enumerate((
+    small = [pltpu.make_async_copy(src, dst, local_sem.at[7 + 2 * layers + i]) for i, (src, dst) in enumerate((
         (hid_any, h_end), (ga_any, ga_raw), (gm_any, gm_raw), (qg_any, qg_raw), (kg_any, kg_raw), (pos_any, pos_ref), (freq_any, freq_ref)))]
     start(small)
     start(qkv_loads(0))
@@ -256,9 +265,8 @@
     score_slot = score_col // kv_heads
     score_own = (score_col % kv_heads == score_head) | (score_head >= kv_heads)
 
-    for d in range(1, n_x):
-        first_copy(d).wait_recv()
-        first_copy(d).wait_send()
+    received(at_first, stat.at[0, 1:n_x])
+    delivered(1, stat.at[0, 1:n_x])
     sums = [along_rows(stat[0, d], x * n_seq) for d in range(n_x)]
     scale = lax.rsqrt(sum(sums) / model_dim + NORM_EPS)
     for d in range(n_x):
@@ -273,8 +281,7 @@
                 start(loads(layer + 1))
 
         reload(qkv_loads)
-        for d in range(1, n_x):
-            qkv_copy(d).wait_recv()
+        received(at_qkv, qkv_recv.at[1:n_x])
 
         def projected(cols, scale_cols):
             total = qkv_part[x, :, cols].astype(F32) * part_scale[0, :, scale_cols]
@@ -299,33 +306,38 @@
 
         finish(cache_loads(layer))
 
-        def sequences(i):
+        def update(i):
             for u in range(SEQS):
                 b = i * SEQS + u
-                slots = slot_ref[b]
-                hit = slot_id == slots[:, :HEAD_DIM]
+                hit = slot_id == slot_ref[b][:, :HEAD_DIM]
                 for j, buf in enumerate((kbuf, vbuf)):
                     fresh = kv_rows[j, 0, b]
                     for h in range(1, kv_heads):
                         fresh = jnp.where(head_id == h, kv_rows[j, h, b], fresh)
                     buf[layer, b] = jnp.where(hit, fresh, buf[layer, b].astype(F32)).astype(BF16)
-                q_b = q_rows[pl.ds(pl.multiple_of(b * 16, 16), 16), :].astype(BF16)
-                scores = lax.dot_general(q_b, kbuf[layer, b], (((1,), (1,)), ((), ())), preferred_element_type=F32) * (HEAD_DIM ** -0.5)
-                scores = jnp.where(score_own & (score_slot <= slots), scores, -1e30)
-                top = jnp.max(scores, axis=1, keepdims=True)
-                e = jnp.exp(scores - top)
-                probs = (e / jnp.sum(e, axis=1, keepdims=True)).astype(BF16)
-                o_rows[pl.ds(pl.multiple_of(b * 16, 16), 16), :] = jnp.dot(probs, vbuf[layer, b], preferred_element_type=F32)
-
-        each(0, n_seq // SEQS, sequences)
+
+        each(0, n_seq // SEQS, update)
+        for b in range(n_seq):
+            q_b = q_rows[b * 16:(b + 1) * 16, :].astype(BF16)
+            scores = lax.dot_general(q_b, kbuf[layer, b], (((1,), (1,)), ((), ())), preferred_element_type=F32) * (HEAD_DIM ** -0.5)
+            s_rows[b * 16:(b + 1) * 16, :] = jnp.where(score_own & (score_slot <= slot_ref[b]), scores, -1e30)
+
+        def softmax(i):
+            block = pl.ds(pl.multiple_of(i * 16 * SEQS, 16 * SEQS), 16 * SEQS)
+            scores = s_rows[block, :]
+            e = jnp.exp(scores - jnp.max(scores, axis=1, keepdims=True))
+            p_rows[block, :] = (e / jnp.sum(e, axis=1, keepdims=True)).astype(BF16)
+
+        each(0, n_seq // SEQS, softmax)
+        for b in range(n_seq):
+            o_rows[b * 16:(b + 1) * 16, :] = jnp.dot(p_rows[b * 16:(b + 1) * 16, :], vbuf[layer, b], preferred_element_type=F32)
         for h in range(q_heads):
             attn_all[x, :, h * HEAD_DIM:(h + 1) * HEAD_DIM] = o_rows[pl.ds(h, n_seq, stride=16), :].astype(BF16)
         for d in (2, 3, 1):
             attn_copy(d).start()
         finish(o_loads(layer))
-        for d in range(1, n_x):
-            qkv_copy(d).wait_send()
-            attn_copy(d).wait_recv()
+        delivered(0, qkv_recv.at[1:n_x])
+        received(at_attn, attn_all.at[1:n_x])
 
         drain_mid = all_reduce(
             0, at_mid, lambda cols: jnp.dot(attn_all[...].reshape(batch, q_cols), wo[:, cols], preferred_element_type=F32), h_end, h_mid, True)
@@ -334,50 +346,59 @@
         normalise(h_mid, 1, gm_ref, layer)
         finish(gate_up_loads(layer))
 
-        def project(s):
-            @pl.when(s < f_tiles)
-            def _():
-                cols = tile_cols(s)
-                gate = jnp.dot(n_buf[...], wg[:, cols], preferred_element_type=F32).astype(BF16)
-                up = jnp.dot(n_buf[...], wu[:, cols], preferred_element_type=F32).astype(BF16)
-                gu_part[0, :, :, :, cols] = gate.reshape(2, 2, rows, TILE)
-                gu_part[1, :, :, :, cols] = up.reshape(2, 2, rows, TILE)
-                pair_copy(s).start()
-
-            @pl.when(s >= PAIR_LAG)
-            def _():
-                t = s - PAIR_LAG
+        def project(t):
+            cols = tile_cols(t)
+            gate = jnp.dot(n_buf[...], wg[:, cols], preferred_element_type=F32).astype(BF16)
+            up = jnp.dot(n_buf[...], wu[:, cols], preferred_element_type=F32).astype(BF16)
+            gu_part[0, :, :, :, cols] = gate.reshape(2, 2, rows, TILE)
+            gu_part[1, :, :, :, cols] = up.reshape(2, 2, rows, TILE)
+
+        def cross(g):
+            cols = group_cols(g)
+            received(at_mlp + g, gu_pair.at[:, :, :, cols])
+
+            def tile(t):
                 cols = tile_cols(t)
-                pair_copy(t).wait_recv()
                 pair = gu_part[:, 1 - chip, core, :, cols].astype(F32) + gu_pair[:, 1 - chip, :, cols].astype(F32)
                 gu_send[:, :, cols] = pair.astype(BF16)
-                across_copy(t).start()
-
-        each(0, f_tiles + PAIR_LAG, project)
+
+            each(*groups[g], tile)
+            across_copy(g).start()
+
+        def activate(g):
+            received(at_mlp + len(groups) + g, gu_recv.at[:, :, group_cols(g)])
+
+            def tile(t):
+                cols = tile_cols(t)
+                gate_up = (gu_part[:, chip, core, :, cols].astype(F32) + gu_pair[:, chip, :, cols].astype(F32)
+                           + gu_recv[:, :, cols].astype(F32)).astype(BF16).astype(F32)
+                act_all[x, :, cols] = (jax.nn.silu(gate_up[0]) * gate_up[1]).astype(BF16)
+
+            each(*groups[g], tile)
+            start(act_copies(g))
+
+        for g in range(len(groups)):
+            each(*groups[g], project)
+            pair_copy(g).start()
+            if g >= 2:
+                cross(g - 2)
         reload(gate_up_loads)
-
-        def activate(t):
-            cols = tile_cols(t)
-            across_copy(t).wait_recv()
-            gate_up = (gu_part[:, chip, core, :, cols].astype(F32) + gu_pair[:, chip, :, cols].astype(F32)
-                       + gu_recv[:, :, cols].astype(F32)).astype(BF16).astype(F32)
-            act_all[x, :, cols] = (jax.nn.silu(gate_up[0]) * gate_up[1]).astype(BF16)
-            start(act_copies(t))
-
-        each(0, f_tiles, activate)
+        for g in range(max(len(groups) - 2, 0), len(groups)):
+            cross(g)
+        for g in range(len(groups)):
+            activate(g)
         drain_mid()
-        for d in range(1, n_x):
-            attn_copy(d).wait_send()
-        acc[...] = jnp.zeros_like(acc)
+        delivered(2, attn_all.at[1:n_x])
         finish(down_loads(layer))
-
-        def down(t):
-            for copy in act_copies(t):
-                copy.wait_recv()
-            vals = act_all[:, :, tile_cols(t)].reshape(batch, TILE)
-            acc[...] += jnp.dot(vals, wd[tile_cols(t), :], preferred_element_type=F32)
-
-        each(0, f_tiles, down)
+        for g, (first, last) in enumerate(groups):
+            cols = group_cols(g)
+            received(at_mlp + 2 * len(groups) + g, act_all.at[1:n_x, :, cols])
+
+            def down(t):
+                part = jnp.dot(act_all[:, :, cols].reshape(batch, (last - first) * TILE), wd[cols, tile_cols(t)], preferred_element_type=F32)
+                acc[:, tile_cols(t)] = acc[:, tile_cols(t)] + part if g else part
+
+            each(0, d_tiles, down)
         reload(down_loads)
         drain_end = all_reduce(1, at_end, lambda cols: acc[:, cols], h_mid, h_end, more)
 
@@ -392,13 +413,9 @@
 
         drain_end()
 
-        def drain_mlp(t):
-            pair_copy(t).wait_send()
-            across_copy(t).wait_send()
-            for copy in act_copies(t):
-                copy.wait_send()
-
-        each(0, f_tiles, drain_mlp)
+        delivered(9, gu_pair)
+        delivered(10, gu_recv)
+        delivered(11, act_all.at[1:n_x])
 
     each(0, layers, run_layer)
     hid_out[...] = h_end[...]
@@ -450,7 +467,7 @@
         cache_shape = (layers, n_seq, slots2, HEAD_DIM)
         peers = n_y * n_x
         d_tiles, f_tiles = depth // TILE, ffn // TILE
-        copies = 3 * (n_x - 1) + 2 * (2 * (n_y - 1) * d_tiles + peers - 1) + 5 * f_tiles
+        receives = 3 + 2 * (d_tiles + 2) + 3 * len(split_tiles(f_tiles))
         positions = positions.reshape(1, batch)
         new_hidden, new_rows = pl.pallas_call(
             functools.partial(step_kernel, dims),
@@ -495,9 +512,11 @@
                 pltpu.VMEM((n_seq, 1, slots2), jnp.int32),
                 pltpu.VMEM((n_x, n_seq, TILE), F32),
                 pltpu.VMEM((2, kv_heads, n_seq, 1, HEAD_DIM), F32),
-                pltpu.SemaphoreType.DMA((copies,)),
-                pltpu.SemaphoreType.DMA((copies,)),
-                pltpu.SemaphoreType.DMA((17 + 2 * layers,)),
+                pltpu.VMEM((16 * n_seq, slots2), F32),
+                pltpu.VMEM((16 * n_seq, slots2), BF16),
+                pltpu.SemaphoreType.DMA((12,)),
+                pltpu.SemaphoreType.DMA((receives,)),
+                pltpu.SemaphoreType.DMA((14 + 2 * layers,)),
             ],
             compiler_params=pltpu.CompilerParams(collective_id=0, has_side_effects=True, vmem_limit_bytes=64 * 1024 * 1024 - 65536),
         )(hidden.reshape(n_y, rows, depth), positions, inverse_frequencies(), g_attn, g_mlp, q_gain, k_gain,

time: 121 us -> 115 us (0.950)
  Pallas kernels: 120 us -> 114 us
    pallas_call x1, Pallas kernels: 116 us -> 110 us  [device_step(): pl.pallas_call(functools.partial(step_kernel, dims), out_shape=(jax.Shape...]
where the time goes in v5:
time: 115 us
  Pallas kernels  114 us (99%)
    pallas_call x1, Pallas kernels, device_step(): pl.pallas_call(functools.partial(step_kernel, dims), out_shape=(jax.Shape...  110 us
    pallas_call x1, Pallas kernels, device_step(): pl.pallas_call(functools.partial(cache_kernel, (layers, n_seq, kv_heads))...  4.23 us

profile of v5, /device:TPU:0, one launch (start us, length us, event | category | flops | bytes accessed | tf_op | source)
XLA Modules:
  0.0 114.8 jit_solution(6047900755584726606)
XLA Ops:
  0.6 110.0 %shard_map.175 = (bf16[4,16,1280]{2,1,0:T(8,128)(2,1)}, f32[2,2,2,16,128]{4,3,2,1,0:T(8,128)}) custom-call(bf16[4,16,1280]{2,1,0:T(8,128)(2,1)} %bitcast.7, s32[1,64]{1,0:T(1,128)} %bitcast.9, f32[1,128]{1,0:T(1,128)} %constant.2.clone.refs_2_, bf16[2,1280]{1,0:T(2,128)(2,1)} %refs_3_.1, bf16[2,1280]{1,0:T(2,128)(2,1)} %refs_4_.1, bf16[2,128]{1,0:T(2,128)(2,1)} %refs_5_.1, ...), custom_call_target="tpu_custom_call" | custom-call | tf_op jit(solution)/shard_map/pallas_call | solution.py:472
  110.6 4.2 %shard_map.176 = (bf16[64,1280]{1,0:T(8,128)(2,1)}, bf16[2,16,128,2,128]{4,3,2,1,0:T(2,128)(2,1)}, bf16[2,16,128,2,128]{4,3,2,1,0:T(2,128)(2,1)}) custom-call(bf16[64,1280]{1,0:T(8,128)(2,1)} %bitcast.8, f32[2,2,2,16,128]{4,3,2,1,0:T(8,128)} %get-tuple-element.6.new_ref, s32[1,64]{1,0:T(1,128)} %bitcast.10, bf16[2,16,128,2,128]{4,3,2,1,0:T(2,128)(2,1)} %kc_ref.1, ...), custom_call_target="tpu_custom_call" | custom-call | tf_op jit(solution)/shard_map/pallas_call | solution.py:524

commit v6 on v5

--- a/solution.py
+++ b/solution.py
@@ -60,9 +60,9 @@
     diagonal = 2 * (1 - chip) + (1 - core)
 
     groups = split_tiles(f_tiles)
-    at_qkv, at_first, at_attn, at_mid = 0, 1, 2, 3
-    at_end = at_mid + d_tiles + 2
-    at_mlp = at_end + d_tiles + 2
+    at_qkv, at_first, at_attn, at_mid = 0, 1, 3, 4
+    at_end = at_mid + d_tiles + 1
+    at_mlp = at_end + d_tiles + 1
 
     def remote(src, dst, to_send, to_recv, to_y, to_x):
         return pltpu.make_async_remote_copy(
@@ -120,19 +120,24 @@
     def along_rows(lanes, first_row):
         return jnp.sum(jnp.where(lane_i == row_i + first_row, lanes, 0.0), axis=1, keepdims=True)
 
-    def normalise(hidden_ref, i, gain_ref, layer):
-        total = jnp.sum(stat[i], axis=0)
-        scales = lax.rsqrt(total / model_dim + NORM_EPS)
-        gain = gain_ref[layer]
-
-        def block(b):
-            n_buf[pl.ds(pl.multiple_of(b * rows, rows), rows), :] = (hidden_ref[b].astype(F32) * along_rows(scales, b * rows) * gain).astype(BF16)
-
-        each(0, n_y, block)
-
-    def all_reduce(i, base, tile_product, residual_ref, result_ref, with_stats):
-        others = n_y - 1
-        send = 3 + 3 * i
+    def local_norm(hidden_ref, gain, i):
+        def block(b, lanes):
+            vals = hidden_ref[b].astype(F32)
+            sums = jnp.sum(vals * vals, axis=1, keepdims=True)
+            n_buf[pl.ds(pl.multiple_of(b * rows, rows), rows), :] = (vals * lax.rsqrt(sums / depth + NORM_EPS) * gain).astype(BF16)
+            return lanes + along_lanes(sums, b * rows)
+
+        stat[i, 0] = lax.fori_loop(0, n_y, block, jnp.zeros((1, HEAD_DIM), F32))
+
+    def corrections(i):
+        total = stat[i, 0]
+        for d in range(1, n_x):
+            total = total + stat[i, d]
+        scale = lax.rsqrt(total / model_dim + NORM_EPS)
+        return lambda d: jnp.where(scale > 0.0, scale / lax.rsqrt(stat[i, d] / depth + NORM_EPS), 0.0)
+
+    def all_reduce(i, base, tile_product, residual_ref, result_ref):
+        send = 4 + 2 * i
 
         def scatter(t, d):
             cols = tile_cols(t)
@@ -141,9 +146,6 @@
         def gather(t, d):
             mine = result_ref.at[y, :, tile_cols(t)]
             return remote(mine, mine, send + 1, base + d_tiles, (y + d) % n_y, x)
-
-        def share(e):
-            return remote(stat.at[i + 1, 0], stat.at[i + 1, e], send + 2, base + d_tiles + 1, (y + e // n_x) % n_y, (x + e % n_x) % n_x)
 
         def send_tile(t):
             ar_part[i, :, :, tile_cols(t)] = tile_product(tile_cols(t)).astype(BF16).reshape(n_y, rows, TILE)
@@ -152,7 +154,7 @@
 
         each(0, d_tiles, send_tile)
 
-        def sum_tile(t, squares):
+        def sum_tile(t):
             cols = tile_cols(t)
             received(base + t, ar_recv.at[i, 1:n_y, :, cols])
             total = ar_part[i, y, :, cols].astype(F32)
@@ -162,36 +164,22 @@
             result_ref[y, :, cols] = new
             for d in (2, 3, 1):
                 gather(t, d).start()
-            return squares + new.astype(F32) * new.astype(F32)
-
-        squares = lax.fori_loop(0, d_tiles, sum_tile, jnp.zeros((rows, TILE), F32))
-        stat[i + 1, 0] = along_lanes(jnp.sum(squares, axis=1, keepdims=True), y * rows)
-
-        @pl.when(with_stats)
-        def _():
-            each(1, peers, lambda e: share(e).start())
-
+
+        each(0, d_tiles, sum_tile)
         received(base + d_tiles, ar_recv.at[i, 1:n_y])
-
-        @pl.when(with_stats)
-        def _():
-            received(base + d_tiles + 1, stat.at[i + 1, 1:peers])
 
         def drain():
             delivered(send, ar_recv.at[i, 1:n_y])
             delivered(send + 1, ar_recv.at[i, 1:n_y])
 
-            @pl.when(with_stats)
-            def _():
-                delivered(send + 2, stat.at[i + 1, 1:peers])
-
         return drain
 
-    def qkv_copy(d):
-        return remote(qkv_part.at[(x + d) % n_x], qkv_recv.at[d], 0, at_qkv, y, (x + d) % n_x)
-
-    def first_copy(d):
-        return remote(stat.at[0, 0], stat.at[0, d], 1, at_first, y, (x + d) % n_x)
+    def qkv_copies(first, last):
+        cols = pl.ds(first * TILE, (last - first) * TILE)
+        return [remote(qkv_part.at[(x + d) % n_x, :, cols], qkv_recv.at[d, :, cols], 0, at_qkv, y, (x + d) % n_x) for d in (2, 3, 1)]
+
+    def sum_copies(i):
+        return [remote(stat.at[i, 0], stat.at[i, d], 1 + 2 * i, at_first + i, y, (x + d) % n_x) for d in (2, 3, 1)]
 
     def attn_copy(d):
         return remote(attn_all.at[x], attn_all.at[x], 2, at_attn, y, (x + d) % n_x)
@@ -211,13 +199,15 @@
         mine = act_all.at[x, :, group_cols(g)]
         return [remote(mine, mine, 11, at_mlp + 2 * len(groups) + g, y, to_x) for to_x in (diagonal, across, partner)]
 
-    def project_qkv():
+    def project_qkv(first, last):
         def tile(t):
             cols = tile_cols(t)
             part = jnp.dot(n_buf[...], wqkv[:, cols], preferred_element_type=F32).astype(BF16)
             qkv_part[:, :, cols] = part.reshape(n_x, n_seq, TILE)
 
-        each(0, qkv_tiles, tile)
+        each(first, last, tile)
+
+    halves = ((0, (qkv_tiles + 1) // 2), ((qkv_tiles + 1) // 2, qkv_tiles))
 
     barrier = pltpu.get_barrier_semaphore()
     each(1, peers, lambda e: pl.semaphore_signal(
@@ -233,21 +223,14 @@
     for raw, wide in ((ga_raw, ga_ref), (gm_raw, gm_ref), (qg_raw, qg_ref), (kg_raw, kg_ref)):
         for layer in range(layers):
             wide[layer] = raw[...].astype(F32)[layer:layer + 1]
-
-    def first_norm(b, lanes):
-        vals = h_end[b].astype(F32)
-        sums = jnp.sum(vals * vals, axis=1, keepdims=True)
-        n_buf[pl.ds(pl.multiple_of(b * rows, rows), rows), :] = (vals * lax.rsqrt(sums / depth + NORM_EPS) * ga_ref[0]).astype(BF16)
-        return lanes + along_lanes(sums, b * rows)
-
-    stat[0, 0] = lax.fori_loop(0, n_y, first_norm, jnp.zeros((1, HEAD_DIM), F32))
+    local_norm(h_end, ga_ref[0], 0)
     q_rows[...] = jnp.zeros_like(q_rows)
     finish(qkv_loads(0))
-    project_qkv()
+    project_qkv(0, qkv_tiles)
     pl.semaphore_wait(barrier, peers - 1)
-    for d in (2, 3, 1):
-        first_copy(d).start()
-        qkv_copy(d).start()
+    start(sum_copies(0))
+    for half in halves:
+        start(qkv_copies(*half))
 
     my_pos = jnp.sum(
         jnp.where(lax.broadcasted_iota(jnp.int32, (n_seq, batch), 1) == lax.broadcasted_iota(jnp.int32, (n_seq, batch), 0) + x * n_seq,
@@ -265,13 +248,6 @@
     score_slot = score_col // kv_heads
     score_own = (score_col % kv_heads == score_head) | (score_head >= kv_heads)
 
-    received(at_first, stat.at[0, 1:n_x])
-    delivered(1, stat.at[0, 1:n_x])
-    sums = [along_rows(stat[0, d], x * n_seq) for d in range(n_x)]
-    scale = lax.rsqrt(sum(sums) / model_dim + NORM_EPS)
-    for d in range(n_x):
-        part_scale[d] = jnp.broadcast_to(jnp.where(scale > 0.0, scale / lax.rsqrt(sums[d] / depth + NORM_EPS), 0.0), (n_seq, TILE))
-
     def run_layer(layer):
         more = layer + 1 < layers
 
@@ -281,6 +257,10 @@
                 start(loads(layer + 1))
 
         reload(qkv_loads)
+        received(at_first, stat.at[0, 1:n_x])
+        correction = corrections(0)
+        for d in range(n_x):
+            part_scale[d] = jnp.broadcast_to(along_rows(correction(d), x * n_seq), (n_seq, TILE))
         received(at_qkv, qkv_recv.at[1:n_x])
 
         def projected(cols, scale_cols):
@@ -337,13 +317,15 @@
             attn_copy(d).start()
         finish(o_loads(layer))
         delivered(0, qkv_recv.at[1:n_x])
+        delivered(1, stat.at[0, 1:n_x])
         received(at_attn, attn_all.at[1:n_x])
 
         drain_mid = all_reduce(
-            0, at_mid, lambda cols: jnp.dot(attn_all[...].reshape(batch, q_cols), wo[:, cols], preferred_element_type=F32), h_end, h_mid, True)
+            0, at_mid, lambda cols: jnp.dot(attn_all[...].reshape(batch, q_cols), wo[:, cols], preferred_element_type=F32), h_end, h_mid)
         reload(o_loads)
 
-        normalise(h_mid, 1, gm_ref, layer)
+        local_norm(h_mid, gm_ref[layer], 1)
+        start(sum_copies(1))
         finish(gate_up_loads(layer))
 
         def project(t):
@@ -359,7 +341,7 @@
 
             def tile(t):
                 cols = tile_cols(t)
-                pair = gu_part[:, 1 - chip, core, :, cols].astype(F32) + gu_pair[:, 1 - chip, :, cols].astype(F32)
+                pair = gu_part[:, 1 - chip, core, :, cols].astype(F32) * part_scale[0] + gu_pair[:, 1 - chip, :, cols].astype(F32) * part_scale[1]
                 gu_send[:, :, cols] = pair.astype(BF16)
 
             each(*groups[g], tile)
@@ -370,7 +352,7 @@
 
             def tile(t):
                 cols = tile_cols(t)
-                gate_up = (gu_part[:, chip, core, :, cols].astype(F32) + gu_pair[:, chip, :, cols].astype(F32)
+                gate_up = (gu_part[:, chip, core, :, cols].astype(F32) * part_scale[2] + gu_pair[:, chip, :, cols].astype(F32) * part_scale[3]
                            + gu_recv[:, :, cols].astype(F32)).astype(BF16).astype(F32)
                 act_all[x, :, cols] = (jax.nn.silu(gate_up[0]) * gate_up[1]).astype(BF16)
 
@@ -380,6 +362,11 @@
         for g in range(len(groups)):
             each(*groups[g], project)
             pair_copy(g).start()
+            if g == 2:
+                received(at_first + 1, stat.at[1, 1:n_x])
+                correction = corrections(1)
+                for i, (d, block) in enumerate(((0, across), (3 - 2 * core, across), (0, x), (3 - 2 * core, x))):
+                    part_scale[i] = jnp.broadcast_to(along_rows(correction(d), block * rows), (rows, TILE))
             if g >= 2:
                 cross(g - 2)
         reload(gate_up_loads)
@@ -400,19 +387,20 @@
 
             each(0, d_tiles, down)
         reload(down_loads)
-        drain_end = all_reduce(1, at_end, lambda cols: acc[:, cols], h_mid, h_end, more)
+        drain_end = all_reduce(1, at_end, lambda cols: acc[:, cols], h_mid, h_end)
 
         @pl.when(more)
         def _():
-            normalise(h_end, 2, ga_ref, layer + 1)
-            part_scale[...] = jnp.ones_like(part_scale)
+            local_norm(h_end, ga_ref[layer + 1], 0)
+            start(sum_copies(0))
             finish(qkv_loads(layer + 1))
-            project_qkv()
-            for d in (2, 3, 1):
-                qkv_copy(d).start()
+            for half in halves:
+                project_qkv(*half)
+                start(qkv_copies(*half))
 
         drain_end()
 
+        delivered(3, stat.at[1, 1:n_x])
         delivered(9, gu_pair)
         delivered(10, gu_recv)
         delivered(11, act_all.at[1:n_x])
@@ -467,7 +455,7 @@
         cache_shape = (layers, n_seq, slots2, HEAD_DIM)
         peers = n_y * n_x
         d_tiles, f_tiles = depth // TILE, ffn // TILE
-        receives = 3 + 2 * (d_tiles + 2) + 3 * len(split_tiles(f_tiles))
+        receives = 4 + 2 * (d_tiles + 1) + 3 * len(split_tiles(f_tiles))
         positions = positions.reshape(1, batch)
         new_hidden, new_rows = pl.pallas_call(
             functools.partial(step_kernel, dims),
@@ -483,7 +471,7 @@
                 pltpu.VMEM(cache_shape, BF16),
                 pltpu.VMEM(cache_shape, BF16),
                 pltpu.VMEM((batch, depth), BF16),
-                pltpu.VMEM((3, peers, 1, HEAD_DIM), F32),
+                pltpu.VMEM((2, n_x, 1, HEAD_DIM), F32),
                 pltpu.VMEM((n_x, n_seq, cols_qkv), BF16),
                 pltpu.VMEM((n_x, n_seq, cols_qkv), BF16),
                 pltpu.VMEM((16 * n_seq, HEAD_DIM), F32),

time: 115 us -> 111 us (0.965)
  Pallas kernels: 114 us -> 110 us
    pallas_call x1, Pallas kernels: 110 us -> 106 us  [device_step(): pl.pallas_call(functools.partial(step_kernel, dims), out_shape=(jax.Shape...]
where the time goes in v6:
time: 111 us
  Pallas kernels  110 us (99%)
    pallas_call x1, Pallas kernels, device_step(): pl.pallas_call(functools.partial(step_kernel, dims), out_shape=(jax.Shape...  106 us
    pallas_call x1, Pallas kernels, device_step(): pl.pallas_call(functools.partial(cache_kernel, (layers, n_seq, kv_heads))...  4.23 us

profile of v6, /device:TPU:0, one launch (start us, length us, event | category | flops | bytes accessed | tf_op | source)
XLA Modules:
  0.0 111.1 jit_solution(8135035960781201612)
XLA Ops:
  0.6 106.2 %shard_map.175 = (bf16[4,16,1280]{2,1,0:T(8,128)(2,1)}, f32[2,2,2,16,128]{4,3,2,1,0:T(8,128)}) custom-call(bf16[4,16,1280]{2,1,0:T(8,128)(2,1)} %bitcast.7, s32[1,64]{1,0:T(1,128)} %bitcast.9, f32[1,128]{1,0:T(1,128)} %constant.2.clone.refs_2_, bf16[2,1280]{1,0:T(2,128)(2,1)} %refs_3_.1, bf16[2,1280]{1,0:T(2,128)(2,1)} %refs_4_.1, bf16[2,128]{1,0:T(2,128)(2,1)} %refs_5_.1, ...), custom_call_target="tpu_custom_call" | custom-call | tf_op jit(solution)/shard_map/pallas_call | solution.py:460
  106.9 4.2 %shard_map.176 = (bf16[64,1280]{1,0:T(8,128)(2,1)}, bf16[2,16,128,2,128]{4,3,2,1,0:T(2,128)(2,1)}, bf16[2,16,128,2,128]{4,3,2,1,0:T(2,128)(2,1)}) custom-call(bf16[64,1280]{1,0:T(8,128)(2,1)} %bitcast.8, f32[2,2,2,16,128]{4,3,2,1,0:T(8,128)} %get-tuple-element.6.new_ref, s32[1,64]{1,0:T(1,128)} %bitcast.10, bf16[2,16,128,2,128]{4,3,2,1,0:T(2,128)(2,1)} %kc_ref.1, ...), custom_call_target="tpu_custom_call" | custom-call | tf_op jit(solution)/shard_map/pallas_call | solution.py:512

commit v7 on v6

--- a/solution.py
+++ b/solution.py
@@ -38,7 +38,7 @@
      hid_out, new_out,
      wqkv, wo, wg, wu, wd, kbuf, vbuf, n_buf, stat, qkv_part, qkv_recv, q_rows, o_rows, attn_all,
      ar_part, ar_recv, h_mid, h_end, gu_part, gu_pair, gu_send, gu_recv, act_all, acc,
-     pos_ref, freq_ref, ga_raw, gm_raw, qg_raw, kg_raw, ga_ref, gm_ref, qg_ref, kg_ref, slot_ref, part_scale, kv_rows, s_rows, p_rows,
+     pos_ref, freq_ref, ga_raw, gm_raw, qg_raw, kg_raw, ga_ref, gm_ref, qg_ref, kg_ref, slot_ref, part_scale, pair_scale, kv_rows, gu_direct, s_rows, p_rows,
      send_sem, recv_sem, local_sem) = refs
     batch = n_y * rows
     cols_qkv = q_cols + 2 * kv_cols
@@ -58,6 +58,7 @@
     partner = 2 * chip + (1 - core)
     across = 2 * (1 - chip) + core
     diagonal = 2 * (1 - chip) + (1 - core)
+    from_partner = 3 - 2 * core
 
     groups = split_tiles(f_tiles)
     at_qkv, at_first, at_attn, at_mid = 0, 1, 3, 4
@@ -195,6 +196,16 @@
         cols = group_cols(g)
         return remote(gu_send.at[:, :, cols], gu_recv.at[:, :, cols], 10, at_mlp + len(groups) + g, y, across)
 
+    tail = len(groups) - 1
+    before = groups[tail][0] * TILE
+
+    def tail_copies():
+        def copy(d):
+            to_x = (x + d) % n_x
+            return remote(gu_part.at[:, to_x // 2, to_x % 2, :, group_cols(tail)], gu_direct.at[d], 8, at_mlp + tail, y, to_x)
+
+        return [copy(d) for d in (2, 3, 1)]
+
     def act_copies(g):
         mine = act_all.at[x, :, group_cols(g)]
         return [remote(mine, mine, 11, at_mlp + 2 * len(groups) + g, y, to_x) for to_x in (diagonal, across, partner)]
@@ -209,23 +220,23 @@
 
     halves = ((0, (qkv_tiles + 1) // 2), ((qkv_tiles + 1) // 2, qkv_tiles))
 
-    barrier = pltpu.get_barrier_semaphore()
-    each(1, peers, lambda e: pl.semaphore_signal(
-        barrier, inc=1, device_id={"y": (y + e // n_x) % n_y, "x": (x + e % n_x) % n_x}, device_id_type=MESH))
     small = [pltpu.make_async_copy(src, dst, local_sem.at[7 + 2 * layers + i]) for i, (src, dst) in enumerate((
         (hid_any, h_end), (ga_any, ga_raw), (gm_any, gm_raw), (qg_any, qg_raw), (kg_any, kg_raw), (pos_any, pos_ref), (freq_any, freq_ref)))]
     start(small)
     start(qkv_loads(0))
+    barrier = pltpu.get_barrier_semaphore()
+    each(1, peers, lambda e: pl.semaphore_signal(
+        barrier, inc=1, device_id={"y": (y + e // n_x) % n_y, "x": (x + e % n_x) % n_x}, device_id_type=MESH))
     finish(small)
-    start(o_loads(0) + cache_loads(0) + gate_up_loads(0) + down_loads(0))
-    for layer in range(1, layers):
-        start(cache_loads(layer))
     for raw, wide in ((ga_raw, ga_ref), (gm_raw, gm_ref), (qg_raw, qg_ref), (kg_raw, kg_ref)):
         for layer in range(layers):
             wide[layer] = raw[...].astype(F32)[layer:layer + 1]
     local_norm(h_end, ga_ref[0], 0)
     q_rows[...] = jnp.zeros_like(q_rows)
     finish(qkv_loads(0))
+    start(cache_loads(0) + o_loads(0) + gate_up_loads(0) + down_loads(0))
+    for layer in range(1, layers):
+        start(cache_loads(layer))
     project_qkv(0, qkv_tiles)
     pl.semaphore_wait(barrier, peers - 1)
     start(sum_copies(0))
@@ -341,7 +352,7 @@
 
             def tile(t):
                 cols = tile_cols(t)
-                pair = gu_part[:, 1 - chip, core, :, cols].astype(F32) * part_scale[0] + gu_pair[:, 1 - chip, :, cols].astype(F32) * part_scale[1]
+                pair = gu_part[:, 1 - chip, core, :, cols].astype(F32) * pair_scale[0] + gu_pair[:, 1 - chip, :, cols].astype(F32) * pair_scale[1]
                 gu_send[:, :, cols] = pair.astype(BF16)
 
             each(*groups[g], tile)
@@ -352,28 +363,47 @@
 
             def tile(t):
                 cols = tile_cols(t)
-                gate_up = (gu_part[:, chip, core, :, cols].astype(F32) * part_scale[2] + gu_pair[:, chip, :, cols].astype(F32) * part_scale[3]
+                gate_up = (gu_part[:, chip, core, :, cols].astype(F32) * part_scale[0] + gu_pair[:, chip, :, cols].astype(F32) * part_scale[from_partner]
                            + gu_recv[:, :, cols].astype(F32)).astype(BF16).astype(F32)
                 act_all[x, :, cols] = (jax.nn.silu(gate_up[0]) * gate_up[1]).astype(BF16)
 
             each(*groups[g], tile)
             start(act_copies(g))
 
+        def activate_tail():
+            received(at_mlp + tail, gu_direct.at[1:n_x])
+
+            def tile(t):
+                cols = tile_cols(t)
+                total = gu_part[:, chip, core, :, cols].astype(F32) * part_scale[0]
+                for d in range(1, n_x):
+                    total = total + gu_direct[d, :, :, tile_cols(t - groups[tail][0])].astype(F32) * part_scale[d]
+                gate_up = total.astype(BF16).astype(F32)
+                act_all[x, :, cols] = (jax.nn.silu(gate_up[0]) * gate_up[1]).astype(BF16)
+
+            each(*groups[tail], tile)
+            start(act_copies(tail))
+
         for g in range(len(groups)):
             each(*groups[g], project)
-            pair_copy(g).start()
+            if g < tail:
+                pair_copy(g).start()
+            else:
+                start(tail_copies())
             if g == 2:
                 received(at_first + 1, stat.at[1, 1:n_x])
                 correction = corrections(1)
-                for i, (d, block) in enumerate(((0, across), (3 - 2 * core, across), (0, x), (3 - 2 * core, x))):
-                    part_scale[i] = jnp.broadcast_to(along_rows(correction(d), block * rows), (rows, TILE))
+                for d in range(n_x):
+                    part_scale[d] = jnp.broadcast_to(along_rows(correction(d), x * rows), (rows, TILE))
+                for i, d in enumerate((0, from_partner)):
+                    pair_scale[i] = jnp.broadcast_to(along_rows(correction(d), across * rows), (rows, TILE))
             if g >= 2:
                 cross(g - 2)
         reload(gate_up_loads)
-        for g in range(max(len(groups) - 2, 0), len(groups)):
-            cross(g)
-        for g in range(len(groups)):
+        cross(tail - 1)
+        for g in range(tail):
             activate(g)
+        activate_tail()
         drain_mid()
         delivered(2, attn_all.at[1:n_x])
         finish(down_loads(layer))
@@ -401,8 +431,9 @@
         drain_end()
 
         delivered(3, stat.at[1, 1:n_x])
-        delivered(9, gu_pair)
-        delivered(10, gu_recv)
+        delivered(8, gu_direct.at[1:n_x])
+        delivered(9, gu_pair.at[:, :, :, 0:before])
+        delivered(10, gu_recv.at[:, :, 0:before])
         delivered(11, act_all.at[1:n_x])
 
     each(0, layers, run_layer)
@@ -499,7 +530,9 @@
                 pltpu.VMEM((layers, 1, HEAD_DIM), F32),
                 pltpu.VMEM((n_seq, 1, slots2), jnp.int32),
                 pltpu.VMEM((n_x, n_seq, TILE), F32),
+                pltpu.VMEM((2, rows, TILE), F32),
                 pltpu.VMEM((2, kv_heads, n_seq, 1, HEAD_DIM), F32),
+                pltpu.VMEM((n_x, 2, rows, (split_tiles(f_tiles)[-1][1] - split_tiles(f_tiles)[-1][0]) * TILE), BF16),
                 pltpu.VMEM((16 * n_seq, slots2), F32),
                 pltpu.VMEM((16 * n_seq, slots2), BF16),
                 pltpu.SemaphoreType.DMA((12,)),

time: 111 us -> 113 us (1.018)
  Pallas kernels: 110 us -> 112 us
    pallas_call x1, Pallas kernels: 106 us -> 108 us  [device_step(): pl.pallas_call(functools.partial(step_kernel, dims), out_shape=(jax.Shape...]
where the time goes in v7:
time: 113 us
  Pallas kernels  112 us (99%)
    pallas_call x1, Pallas kernels, device_step(): pl.pallas_call(functools.partial(step_kernel, dims), out_shape=(jax.Shape...  108 us
    pallas_call x1, Pallas kernels, device_step(): pl.pallas_call(functools.partial(cache_kernel, (layers, n_seq, kv_heads))...  4.23 us

profile of v7, /device:TPU:0, one launch (start us, length us, event | category | flops | bytes accessed | tf_op | source)
XLA Modules:
  0.0 112.6 jit_solution(6213604014081561531)
XLA Ops:
  0.6 107.7 %shard_map.175 = (bf16[4,16,1280]{2,1,0:T(8,128)(2,1)}, f32[2,2,2,16,128]{4,3,2,1,0:T(8,128)}) custom-call(bf16[4,16,1280]{2,1,0:T(8,128)(2,1)} %bitcast.7, s32[1,64]{1,0:T(1,128)} %bitcast.9, f32[1,128]{1,0:T(1,128)} %constant.2.clone.refs_2_, bf16[2,1280]{1,0:T(2,128)(2,1)} %refs_3_.1, bf16[2,1280]{1,0:T(2,128)(2,1)} %refs_4_.1, bf16[2,128]{1,0:T(2,128)(2,1)} %refs_5_.1, ...), custom_call_target="tpu_custom_call" | custom-call | tf_op jit(solution)/shard_map/pallas_call | solution.py:491
  108.3 4.2 %shard_map.176 = (bf16[64,1280]{1,0:T(8,128)(2,1)}, bf16[2,16,128,2,128]{4,3,2,1,0:T(2,128)(2,1)}, bf16[2,16,128,2,128]{4,3,2,1,0:T(2,128)(2,1)}) custom-call(bf16[64,1280]{1,0:T(8,128)(2,1)} %bitcast.8, f32[2,2,2,16,128]{4,3,2,1,0:T(8,128)} %get-tuple-element.6.new_ref, s32[1,64]{1,0:T(1,128)} %bitcast.10, bf16[2,16,128,2,128]{4,3,2,1,0:T(2,128)(2,1)} %kc_ref.1, ...), custom_call_target="tpu_custom_call" | custom-call | tf_op jit(solution)/shard_map/pallas_call | solution.py:545

commit v8 on v6

--- a/solution.py
+++ b/solution.py
@@ -195,9 +195,19 @@
         cols = group_cols(g)
         return remote(gu_send.at[:, :, cols], gu_recv.at[:, :, cols], 10, at_mlp + len(groups) + g, y, across)
 
+    tail = len(groups) - 1
+    at_act = at_mlp + 2 * len(groups)
+    at_crossed = at_act + len(groups)
+
     def act_copies(g):
         mine = act_all.at[x, :, group_cols(g)]
-        return [remote(mine, mine, 11, at_mlp + 2 * len(groups) + g, y, to_x) for to_x in (diagonal, across, partner)]
+        crossing = remote(mine, mine, 11, at_crossed + g if g < tail else at_act + g, y, across)
+        return [crossing] + [remote(mine, mine, 11, at_act + g, y, to_x) for to_x in ((partner,) if g < tail else (diagonal, partner))]
+
+    def pass_on(g):
+        theirs = act_all.at[across, :, group_cols(g)]
+        received(at_crossed + g, theirs)
+        remote(theirs, theirs, 11, at_act + g, y, partner).start()
 
     def project_qkv(first, last):
         def tile(t):
@@ -209,23 +219,23 @@
 
     halves = ((0, (qkv_tiles + 1) // 2), ((qkv_tiles + 1) // 2, qkv_tiles))
 
-    barrier = pltpu.get_barrier_semaphore()
-    each(1, peers, lambda e: pl.semaphore_signal(
-        barrier, inc=1, device_id={"y": (y + e // n_x) % n_y, "x": (x + e % n_x) % n_x}, device_id_type=MESH))
     small = [pltpu.make_async_copy(src, dst, local_sem.at[7 + 2 * layers + i]) for i, (src, dst) in enumerate((
         (hid_any, h_end), (ga_any, ga_raw), (gm_any, gm_raw), (qg_any, qg_raw), (kg_any, kg_raw), (pos_any, pos_ref), (freq_any, freq_ref)))]
     start(small)
     start(qkv_loads(0))
+    barrier = pltpu.get_barrier_semaphore()
+    each(1, peers, lambda e: pl.semaphore_signal(
+        barrier, inc=1, device_id={"y": (y + e // n_x) % n_y, "x": (x + e % n_x) % n_x}, device_id_type=MESH))
     finish(small)
-    start(o_loads(0) + cache_loads(0) + gate_up_loads(0) + down_loads(0))
-    for layer in range(1, layers):
-        start(cache_loads(layer))
     for raw, wide in ((ga_raw, ga_ref), (gm_raw, gm_ref), (qg_raw, qg_ref), (kg_raw, kg_ref)):
         for layer in range(layers):
             wide[layer] = raw[...].astype(F32)[layer:layer + 1]
     local_norm(h_end, ga_ref[0], 0)
     q_rows[...] = jnp.zeros_like(q_rows)
     finish(qkv_loads(0))
+    start(cache_loads(0) + o_loads(0) + gate_up_loads(0) + down_loads(0))
+    for layer in range(1, layers):
+        start(cache_loads(layer))
     project_qkv(0, qkv_tiles)
     pl.semaphore_wait(barrier, peers - 1)
     start(sum_copies(0))
@@ -372,20 +382,29 @@
         reload(gate_up_loads)
         for g in range(max(len(groups) - 2, 0), len(groups)):
             cross(g)
+        def down(g):
+            cols = group_cols(g)
+            first, last = groups[g]
+            received(at_act + g, act_all.at[1:3 if g < tail else n_x, :, cols])
+
+            def tile(t):
+                part = jnp.dot(act_all[:, :, cols].reshape(batch, (last - first) * TILE), wd[cols, tile_cols(t)], preferred_element_type=F32)
+                acc[:, tile_cols(t)] = acc[:, tile_cols(t)] + part if g else part
+
+            each(0, d_tiles, tile)
+
         for g in range(len(groups)):
             activate(g)
+            if g >= 3:
+                pass_on(g - 3)
         drain_mid()
         delivered(2, attn_all.at[1:n_x])
         finish(down_loads(layer))
-        for g, (first, last) in enumerate(groups):
-            cols = group_cols(g)
-            received(at_mlp + 2 * len(groups) + g, act_all.at[1:n_x, :, cols])
-
-            def down(t):
-                part = jnp.dot(act_all[:, :, cols].reshape(batch, (last - first) * TILE), wd[cols, tile_cols(t)], preferred_element_type=F32)
-                acc[:, tile_cols(t)] = acc[:, tile_cols(t)] + part if g else part
-
-            each(0, d_tiles, down)
+        waiting = list(range(max(len(groups) - 3, 0), tail))
+        for g in range(len(groups)):
+            if waiting:
+                pass_on(waiting.pop(0))
+            down(g)
         reload(down_loads)
         drain_end = all_reduce(1, at_end, lambda cols: acc[:, cols], h_mid, h_end)
 
@@ -455,7 +474,7 @@
         cache_shape = (layers, n_seq, slots2, HEAD_DIM)
         peers = n_y * n_x
         d_tiles, f_tiles = depth // TILE, ffn // TILE
-        receives = 4 + 2 * (d_tiles + 1) + 3 * len(split_tiles(f_tiles))
+        receives = 4 + 2 * (d_tiles + 1) + 4 * len(split_tiles(f_tiles))
         positions = positions.reshape(1, batch)
         new_hidden, new_rows = pl.pallas_call(
             functools.partial(step_kernel, dims),

time: 111 us -> 113 us (1.018)
  Pallas kernels: 110 us -> 113 us
    pallas_call x1, Pallas kernels: 106 us -> 108 us  [device_step(): pl.pallas_call(functools.partial(step_kernel, dims), out_shape=(jax.Shape...]
where the time goes in v8:
time: 113 us
  Pallas kernels  113 us (100%)
    pallas_call x1, Pallas kernels, device_step(): pl.pallas_call(functools.partial(step_kernel, dims), out_shape=(jax.Shape...  108 us
    pallas_call x1, Pallas kernels, device_step(): pl.pallas_call(functools.partial(cache_kernel, (layers, n_seq, kv_heads))...  4.23 us

profile of v8, /device:TPU:0, one launch (start us, length us, event | category | flops | bytes accessed | tf_op | source)
XLA Modules:
  0.0 113.2 jit_solution(14855194525376473789)
XLA Ops:
  0.6 108.4 %shard_map.175 = (bf16[4,16,1280]{2,1,0:T(8,128)(2,1)}, f32[2,2,2,16,128]{4,3,2,1,0:T(8,128)}) custom-call(bf16[4,16,1280]{2,1,0:T(8,128)(2,1)} %bitcast.7, s32[1,64]{1,0:T(1,128)} %bitcast.9, f32[1,128]{1,0:T(1,128)} %constant.2.clone.refs_2_, bf16[2,1280]{1,0:T(2,128)(2,1)} %refs_3_.1, bf16[2,1280]{1,0:T(2,128)(2,1)} %refs_4_.1, bf16[2,128]{1,0:T(2,128)(2,1)} %refs_5_.1, ...), custom_call_target="tpu_custom_call" | custom-call | tf_op jit(solution)/shard_map/pallas_call | solution.py:479
  109.0 4.2 %shard_map.176 = (bf16[64,1280]{1,0:T(8,128)(2,1)}, bf16[2,16,128,2,128]{4,3,2,1,0:T(2,128)(2,1)}, bf16[2,16,128,2,128]{4,3,2,1,0:T(2,128)(2,1)}) custom-call(bf16[64,1280]{1,0:T(8,128)(2,1)} %bitcast.8, f32[2,2,2,16,128]{4,3,2,1,0:T(8,128)} %get-tuple-element.6.new_ref, s32[1,64]{1,0:T(1,128)} %bitcast.10, bf16[2,16,128,2,128]{4,3,2,1,0:T(2,128)(2,1)} %kc_ref.1, ...), custom_call_target="tpu_custom_call" | custom-call | tf_op jit(solution)/shard_map/pallas_call | solution.py:531

commit v9 on v7

--- a/solution.py
+++ b/solution.py
@@ -94,14 +94,19 @@
     def o_loads(layer):
         return [pltpu.make_async_copy(wo_ref.at[layer], wo, local_sem.at[3])]
 
-    def gate_up_loads(layer):
-        return [pltpu.make_async_copy(src.at[layer], dst, local_sem.at[4 + i]) for i, (src, dst) in enumerate(((wg_ref, wg), (wu_ref, wu)))]
+    def gate_up_loads(layer, piece):
+        first, last = groups[2 * piece][0], groups[min(2 * piece + 1, len(groups) - 1)][1]
+        cols = pl.ds(first * TILE, (last - first) * TILE)
+        return [pltpu.make_async_copy(src.at[layer, :, cols], dst.at[:, cols], local_sem.at[5 + 2 * piece + i])
+                for i, (src, dst) in enumerate(((wg_ref, wg), (wu_ref, wu)))]
+
+    pieces = range((len(groups) + 1) // 2)
 
     def down_loads(layer):
-        return [pltpu.make_async_copy(wd_ref.at[layer], wd, local_sem.at[6])]
+        return [pltpu.make_async_copy(wd_ref.at[layer], wd, local_sem.at[4])]
 
     def cache_loads(layer):
-        return [pltpu.make_async_copy(src.at[layer], dst.at[layer], local_sem.at[7 + i * layers + layer])
+        return [pltpu.make_async_copy(src.at[layer], dst.at[layer], local_sem.at[5 + 2 * len(pieces) + i * layers + layer])
                 for i, (src, dst) in enumerate(((kc_ref, kbuf), (vc_ref, vbuf)))]
 
     def start(copies):
@@ -220,7 +225,7 @@
 
     halves = ((0, (qkv_tiles + 1) // 2), ((qkv_tiles + 1) // 2, qkv_tiles))
 
-    small = [pltpu.make_async_copy(src, dst, local_sem.at[7 + 2 * layers + i]) for i, (src, dst) in enumerate((
+    small = [pltpu.make_async_copy(src, dst, local_sem.at[5 + 2 * len(pieces) + 2 * layers + i]) for i, (src, dst) in enumerate((
         (hid_any, h_end), (ga_any, ga_raw), (gm_any, gm_raw), (qg_any, qg_raw), (kg_any, kg_raw), (pos_any, pos_ref), (freq_any, freq_ref)))]
     start(small)
     start(qkv_loads(0))
@@ -228,16 +233,19 @@
     each(1, peers, lambda e: pl.semaphore_signal(
         barrier, inc=1, device_id={"y": (y + e // n_x) % n_y, "x": (x + e % n_x) % n_x}, device_id_type=MESH))
     finish(small)
+    start(cache_loads(0) + o_loads(0))
+    for piece in pieces:
+        start(gate_up_loads(0, piece))
     for raw, wide in ((ga_raw, ga_ref), (gm_raw, gm_ref), (qg_raw, qg_ref), (kg_raw, kg_ref)):
         for layer in range(layers):
             wide[layer] = raw[...].astype(F32)[layer:layer + 1]
     local_norm(h_end, ga_ref[0], 0)
     q_rows[...] = jnp.zeros_like(q_rows)
     finish(qkv_loads(0))
-    start(cache_loads(0) + o_loads(0) + gate_up_loads(0) + down_loads(0))
+    project_qkv(0, qkv_tiles)
+    start(down_loads(0))
     for layer in range(1, layers):
         start(cache_loads(layer))
-    project_qkv(0, qkv_tiles)
     pl.semaphore_wait(barrier, peers - 1)
     start(sum_copies(0))
     for half in halves:
@@ -337,7 +345,6 @@
 
         local_norm(h_mid, gm_ref[layer], 1)
         start(sum_copies(1))
-        finish(gate_up_loads(layer))
 
         def project(t):
             cols = tile_cols(t)
@@ -385,6 +392,8 @@
             start(act_copies(tail))
 
         for g in range(len(groups)):
+            if g % 2 == 0:
+                finish(gate_up_loads(layer, g // 2))
             each(*groups[g], project)
             if g < tail:
                 pair_copy(g).start()
@@ -399,7 +408,8 @@
                     pair_scale[i] = jnp.broadcast_to(along_rows(correction(d), across * rows), (rows, TILE))
             if g >= 2:
                 cross(g - 2)
-        reload(gate_up_loads)
+        for piece in pieces:
+            reload(lambda layer: gate_up_loads(layer, piece))
         cross(tail - 1)
         for g in range(tail):
             activate(g)
@@ -537,7 +547,7 @@
                 pltpu.VMEM((16 * n_seq, slots2), BF16),
                 pltpu.SemaphoreType.DMA((12,)),
                 pltpu.SemaphoreType.DMA((receives,)),
-                pltpu.SemaphoreType.DMA((14 + 2 * layers,)),
+                pltpu.SemaphoreType.DMA((12 + 2 * ((len(split_tiles(f_tiles)) + 1) // 2) + 2 * layers,)),
             ],
             compiler_params=pltpu.CompilerParams(collective_id=0, has_side_effects=True, vmem_limit_bytes=64 * 1024 * 1024 - 65536),
         )(hidden.reshape(n_y, rows, depth), positions, inverse_frequencies(), g_attn, g_mlp, q_gain, k_gain,

time: 113 us -> 113 us (level)
  no operation moved by 1% of the time
where the time goes in v9:
time: 113 us
  Pallas kernels  112 us (99%)
    pallas_call x1, Pallas kernels, device_step(): pl.pallas_call(functools.partial(step_kernel, dims), out_shape=(jax.Shape...  108 us
    pallas_call x1, Pallas kernels, device_step(): pl.pallas_call(functools.partial(cache_kernel, (layers, n_seq, kv_heads))...  4.23 us

profile of v9, /device:TPU:0, one launch (start us, length us, event | category | flops | bytes accessed | tf_op | source)
XLA Modules:
  0.0 112.6 jit_solution(14876259240658068969)
XLA Ops:
  0.6 107.8 %shard_map.175 = (bf16[4,16,1280]{2,1,0:T(8,128)(2,1)}, f32[2,2,2,16,128]{4,3,2,1,0:T(8,128)}) custom-call(bf16[4,16,1280]{2,1,0:T(8,128)(2,1)} %bitcast.7, s32[1,64]{1,0:T(1,128)} %bitcast.9, f32[1,128]{1,0:T(1,128)} %constant.2.clone.refs_2_, bf16[2,1280]{1,0:T(2,128)(2,1)} %refs_3_.1, bf16[2,1280]{1,0:T(2,128)(2,1)} %refs_4_.1, bf16[2,128]{1,0:T(2,128)(2,1)} %refs_5_.1, ...), custom_call_target="tpu_custom_call" | custom-call | tf_op jit(solution)/shard_map/pallas_call | solution.py:501
  108.4 4.2 %shard_map.176 = (bf16[64,1280]{1,0:T(8,128)(2,1)}, bf16[2,16,128,2,128]{4,3,2,1,0:T(2,128)(2,1)}, bf16[2,16,128,2,128]{4,3,2,1,0:T(2,128)(2,1)}) custom-call(bf16[64,1280]{1,0:T(8,128)(2,1)} %bitcast.8, f32[2,2,2,16,128]{4,3,2,1,0:T(8,128)} %get-tuple-element.6.new_ref, s32[1,64]{1,0:T(1,128)} %bitcast.10, bf16[2,16,128,2,128]{4,3,2,1,0:T(2,128)(2,1)} %kc_ref.1, ...), custom_call_target="tpu_custom_call" | custom-call | tf_op jit(solution)/shard_map/pallas_call | solution.py:555

commit v10 on v9

--- a/solution.py
+++ b/solution.py
@@ -225,13 +225,13 @@
 
     halves = ((0, (qkv_tiles + 1) // 2), ((qkv_tiles + 1) // 2, qkv_tiles))
 
+    barrier = pltpu.get_barrier_semaphore()
+    each(1, peers, lambda e: pl.semaphore_signal(
+        barrier, inc=1, device_id={"y": (y + e // n_x) % n_y, "x": (x + e % n_x) % n_x}, device_id_type=MESH))
     small = [pltpu.make_async_copy(src, dst, local_sem.at[5 + 2 * len(pieces) + 2 * layers + i]) for i, (src, dst) in enumerate((
         (hid_any, h_end), (ga_any, ga_raw), (gm_any, gm_raw), (qg_any, qg_raw), (kg_any, kg_raw), (pos_any, pos_ref), (freq_any, freq_ref)))]
     start(small)
     start(qkv_loads(0))
-    barrier = pltpu.get_barrier_semaphore()
-    each(1, peers, lambda e: pl.semaphore_signal(
-        barrier, inc=1, device_id={"y": (y + e // n_x) % n_y, "x": (x + e % n_x) % n_x}, device_id_type=MESH))
     finish(small)
     start(cache_loads(0) + o_loads(0))
     for piece in pieces:
@@ -408,12 +408,12 @@
                     pair_scale[i] = jnp.broadcast_to(along_rows(correction(d), across * rows), (rows, TILE))
             if g >= 2:
                 cross(g - 2)
-        for piece in pieces:
-            reload(lambda layer: gate_up_loads(layer, piece))
         cross(tail - 1)
         for g in range(tail):
             activate(g)
         activate_tail()
+        for piece in pieces:
+            reload(lambda layer: gate_up_loads(layer, piece))
         drain_mid()
         delivered(2, attn_all.at[1:n_x])
         finish(down_loads(layer))

time: 113 us -> 113 us (level)
  no operation moved by 1% of the time
where the time goes in v10:
time: 113 us
  Pallas kernels  112 us (99%)
    pallas_call x1, Pallas kernels, device_step(): pl.pallas_call(functools.partial(step_kernel, dims), out_shape=(jax.Shape...  108 us
    pallas_call x1, Pallas kernels, device_step(): pl.pallas_call(functools.partial(cache_kernel, (layers, n_seq, kv_heads))...  4.23 us

profile of v10, /device:TPU:0, one launch (start us, length us, event | category | flops | bytes accessed | tf_op | source)
XLA Modules:
  0.0 112.9 jit_solution(18180138571821549978)
XLA Ops:
  0.6 108.0 %shard_map.175 = (bf16[4,16,1280]{2,1,0:T(8,128)(2,1)}, f32[2,2,2,16,128]{4,3,2,1,0:T(8,128)}) custom-call(bf16[4,16,1280]{2,1,0:T(8,128)(2,1)} %bitcast.7, s32[1,64]{1,0:T(1,128)} %bitcast.9, f32[1,128]{1,0:T(1,128)} %constant.2.clone.refs_2_, bf16[2,1280]{1,0:T(2,128)(2,1)} %refs_3_.1, bf16[2,1280]{1,0:T(2,128)(2,1)} %refs_4_.1, bf16[2,128]{1,0:T(2,128)(2,1)} %refs_5_.1, ...), custom_call_target="tpu_custom_call" | custom-call | tf_op jit(solution)/shard_map/pallas_call | solution.py:501
  108.7 4.2 %shard_map.176 = (bf16[64,1280]{1,0:T(8,128)(2,1)}, bf16[2,16,128,2,128]{4,3,2,1,0:T(2,128)(2,1)}, bf16[2,16,128,2,128]{4,3,2,1,0:T(2,128)(2,1)}) custom-call(bf16[64,1280]{1,0:T(8,128)(2,1)} %bitcast.8, f32[2,2,2,16,128]{4,3,2,1,0:T(8,128)} %get-tuple-element.6.new_ref, s32[1,64]{1,0:T(1,128)} %bitcast.10, bf16[2,16,128,2,128]{4,3,2,1,0:T(2,128)(2,1)} %kc_ref.1, ...), custom_call_target="tpu_custom_call" | custom-call | tf_op jit(solution)/shard_map/pallas_call | solution.py:555

commit v11 on v6

--- a/solution.py
+++ b/solution.py
@@ -12,7 +12,7 @@
 NORM_EPS = 1e-6
 ROPE_BASE = 1000000.0
 TILE = 256
-GROUP_TILES = (3, 3, 3, 3, 3, 2)
+GROUP_TILES = (2, 3, 3, 4, 3, 2)
 SEQS = 4
 MESH = pl.DeviceIdType.MESH
 F32 = jnp.float32
@@ -38,7 +38,7 @@
      hid_out, new_out,
      wqkv, wo, wg, wu, wd, kbuf, vbuf, n_buf, stat, qkv_part, qkv_recv, q_rows, o_rows, attn_all,
      ar_part, ar_recv, h_mid, h_end, gu_part, gu_pair, gu_send, gu_recv, act_all, acc,
-     pos_ref, freq_ref, ga_raw, gm_raw, qg_raw, kg_raw, ga_ref, gm_ref, qg_ref, kg_ref, slot_ref, part_scale, kv_rows, s_rows, p_rows,
+     pos_ref, freq_ref, ga_raw, gm_raw, qg_raw, kg_raw, ga_ref, gm_ref, qg_ref, kg_ref, slot_ref, part_scale, pair_scale, kv_rows, s_rows, p_rows,
      send_sem, recv_sem, local_sem) = refs
     batch = n_y * rows
     cols_qkv = q_cols + 2 * kv_cols
@@ -134,7 +134,13 @@
         for d in range(1, n_x):
             total = total + stat[i, d]
         scale = lax.rsqrt(total / model_dim + NORM_EPS)
-        return lambda d: jnp.where(scale > 0.0, scale / lax.rsqrt(stat[i, d] / depth + NORM_EPS), 0.0)
+        return lambda *d: ratio(scale, local_scale(i, *d))
+
+    def local_scale(i, *d):
+        return lax.rsqrt(sum(stat[i, k] for k in d) / (len(d) * depth) + NORM_EPS)
+
+    def ratio(scale, local):
+        return jnp.where(scale > 0.0, scale / local, 0.0)
 
     def all_reduce(i, base, tile_product, residual_ref, result_ref):
         send = 4 + 2 * i
@@ -179,7 +185,10 @@
         return [remote(qkv_part.at[(x + d) % n_x, :, cols], qkv_recv.at[d, :, cols], 0, at_qkv, y, (x + d) % n_x) for d in (2, 3, 1)]
 
     def sum_copies(i):
-        return [remote(stat.at[i, 0], stat.at[i, d], 1 + 2 * i, at_first + i, y, (x + d) % n_x) for d in (2, 3, 1)]
+        if i == 0:
+            return [remote(stat.at[0, 0], stat.at[0, d], 1, at_first, y, (x + d) % n_x) for d in (2, 3, 1)]
+        return [remote(stat.at[1, 0], stat.at[1, k], 3, at_first + 1 if k > 1 else at_mlp + 3 * len(groups), y, to_x)
+                for k, to_x in ((1, partner), (2, across), (3, diagonal))]
 
     def attn_copy(d):
         return remote(attn_all.at[x], attn_all.at[x], 2, at_attn, y, (x + d) % n_x)
@@ -341,7 +350,7 @@
 
             def tile(t):
                 cols = tile_cols(t)
-                pair = gu_part[:, 1 - chip, core, :, cols].astype(F32) * part_scale[0] + gu_pair[:, 1 - chip, :, cols].astype(F32) * part_scale[1]
+                pair = gu_part[:, 1 - chip, core, :, cols].astype(F32) * pair_scale[0] + gu_pair[:, 1 - chip, :, cols].astype(F32) * pair_scale[1]
                 gu_send[:, :, cols] = pair.astype(BF16)
 
             each(*groups[g], tile)
@@ -352,8 +361,8 @@
 
             def tile(t):
                 cols = tile_cols(t)
-                gate_up = (gu_part[:, chip, core, :, cols].astype(F32) * part_scale[2] + gu_pair[:, chip, :, cols].astype(F32) * part_scale[3]
-                           + gu_recv[:, :, cols].astype(F32)).astype(BF16).astype(F32)
+                gate_up = (gu_part[:, chip, core, :, cols].astype(F32) * part_scale[0] + gu_pair[:, chip, :, cols].astype(F32) * part_scale[1]
+                           + gu_recv[:, :, cols].astype(F32) * part_scale[2]).astype(BF16).astype(F32)
                 act_all[x, :, cols] = (jax.nn.silu(gate_up[0]) * gate_up[1]).astype(BF16)
 
             each(*groups[g], tile)
@@ -363,15 +372,19 @@
             each(*groups[g], project)
             pair_copy(g).start()
             if g == 2:
-                received(at_first + 1, stat.at[1, 1:n_x])
-                correction = corrections(1)
-                for i, (d, block) in enumerate(((0, across), (3 - 2 * core, across), (0, x), (3 - 2 * core, x))):
-                    part_scale[i] = jnp.broadcast_to(along_rows(correction(d), block * rows), (rows, TILE))
+                received(at_mlp + 3 * len(groups), stat.at[1, 1:2])
+                for k in range(2):
+                    column = along_rows(ratio(local_scale(1, 0, 1), local_scale(1, k)), across * rows)
+                    pair_scale[k] = jnp.broadcast_to(column, (rows, TILE))
             if g >= 2:
                 cross(g - 2)
         reload(gate_up_loads)
         for g in range(max(len(groups) - 2, 0), len(groups)):
             cross(g)
+        received(at_first + 1, stat.at[1, 2:4])
+        correction = corrections(1)
+        for k, sources in enumerate(((0,), (1,), (2, 3))):
+            part_scale[k] = jnp.broadcast_to(along_rows(correction(*sources), x * rows), (rows, TILE))
         for g in range(len(groups)):
             activate(g)
         drain_mid()
@@ -455,7 +468,7 @@
         cache_shape = (layers, n_seq, slots2, HEAD_DIM)
         peers = n_y * n_x
         d_tiles, f_tiles = depth // TILE, ffn // TILE
-        receives = 4 + 2 * (d_tiles + 1) + 3 * len(split_tiles(f_tiles))
+        receives = 4 + 2 * (d_tiles + 1) + 3 * len(split_tiles(f_tiles)) + 1
         positions = positions.reshape(1, batch)
         new_hidden, new_rows = pl.pallas_call(
             functools.partial(step_kernel, dims),
@@ -499,6 +512,7 @@
                 pltpu.VMEM((layers, 1, HEAD_DIM), F32),
                 pltpu.VMEM((n_seq, 1, slots2), jnp.int32),
                 pltpu.VMEM((n_x, n_seq, TILE), F32),
+                pltpu.VMEM((2, rows, TILE), F32),
                 pltpu.VMEM((2, kv_heads, n_seq, 1, HEAD_DIM), F32),
                 pltpu.VMEM((16 * n_seq, slots2), F32),
                 pltpu.VMEM((16 * n_seq, slots2), BF16),

time: 111 us -> 112 us (level)
  Pallas kernels: 110 us -> 112 us
where the time goes in v11:
time: 112 us
  Pallas kernels  112 us (100%)
    pallas_call x1, Pallas kernels, device_step(): pl.pallas_call(functools.partial(step_kernel, dims), out_shape=(jax.Shape...  107 us
    pallas_call x1, Pallas kernels, device_step(): pl.pallas_call(functools.partial(cache_kernel, (layers, n_seq, kv_heads))...  4.23 us

profile of v11, /device:TPU:0, one launch (start us, length us, event | category | flops | bytes accessed | tf_op | source)
XLA Modules:
  0.0 112.2 jit_solution(3427471664464554126)
XLA Ops:
  0.6 107.3 %shard_map.175 = (bf16[4,16,1280]{2,1,0:T(8,128)(2,1)}, f32[2,2,2,16,128]{4,3,2,1,0:T(8,128)}) custom-call(bf16[4,16,1280]{2,1,0:T(8,128)(2,1)} %bitcast.7, s32[1,64]{1,0:T(1,128)} %bitcast.9, f32[1,128]{1,0:T(1,128)} %constant.2.clone.refs_2_, bf16[2,1280]{1,0:T(2,128)(2,1)} %refs_3_.1, bf16[2,1280]{1,0:T(2,128)(2,1)} %refs_4_.1, bf16[2,128]{1,0:T(2,128)(2,1)} %refs_5_.1, ...), custom_call_target="tpu_custom_call" | custom-call | tf_op jit(solution)/shard_map/pallas_call | solution.py:473
  108.0 4.2 %shard_map.176 = (bf16[64,1280]{1,0:T(8,128)(2,1)}, bf16[2,16,128,2,128]{4,3,2,1,0:T(2,128)(2,1)}, bf16[2,16,128,2,128]{4,3,2,1,0:T(2,128)(2,1)}) custom-call(bf16[64,1280]{1,0:T(8,128)(2,1)} %bitcast.8, f32[2,2,2,16,128]{4,3,2,1,0:T(8,128)} %get-tuple-element.6.new_ref, s32[1,64]{1,0:T(1,128)} %bitcast.10, bf16[2,16,128,2,128]{4,3,2,1,0:T(2,128)(2,1)} %kc_ref.1, ...), custom_call_target="tpu_custom_call" | custom-call | tf_op jit(solution)/shard_map/pallas_call | solution.py:526
